TPU v7x, 32 devices: a whole 2x2x4 slice. The times are simulated.
32 devices in a mesh: dp: 8 (over z, x), tensor: 4 (over y, core).
Axes of the slice: x: 2, y: 2, z: 4, core: 2. Of those that a mesh axis runs over, the one named last changes fastest.
Arguments:
- tokens: bfloat16 [4096, 1536], P(('dp', 'tensor')), may hold values from -6 to 6
- cotangent: bfloat16 [4096, 1536], P(('dp', 'tensor')), may hold values from -6 to 6
- gain_attn: float32 [1536], replicated, may hold values from 0.5 to 1.5
- w_query: bfloat16 [1536, 768], P(None, 'tensor'), may hold values from -0.0546875 to 0.0546875
- w_key: bfloat16 [1536, 768], P(None, 'tensor'), may hold values from -0.0546875 to 0.0546875
- w_value: bfloat16 [1536, 768], P(None, 'tensor'), may hold values from -0.15625 to 0.15625
- w_out: bfloat16 [768, 1536], P('tensor'), may hold values from -3.5 to 3.5
- bias_table: float32 [32, 12], P(None, 'tensor'), may hold values from -4 to 4
- gain_ffn: float32 [1536], replicated, may hold values from 0.5 to 1.5
- w_gate: bfloat16 [1536, 3968], P(None, 'tensor'), may hold values from -0.15625 to 0.15625
- w_up: bfloat16 [1536, 3968], P(None, 'tensor'), may hold values from -0.15625 to 0.15625
- w_down: bfloat16 [3968, 1536], P('tensor'), may hold values from -0.09375 to 0.09375
- lengths: int32 [8, 4], P('dp'), may hold values from 1 to 256, 512 in all within a row
- buckets: int32 [1023], replicated, may hold values from 0 to 31
Outputs:
- block_out: bfloat16 [4096, 1536], P(('dp', 'tensor'))
- grad_tokens: bfloat16 [4096, 1536], P(('dp', 'tensor'))
- grad_gain_attn: float32 [1536], replicated
- grad_w_query: float32 [1536, 768], P(None, 'tensor')
- grad_w_key: float32 [1536, 768], P(None, 'tensor')
- grad_w_value: float32 [1536, 768], P(None, 'tensor')
- grad_w_out: float32 [768, 1536], P('tensor')
- grad_bias_table: float32 [32, 12], P(None, 'tensor')
- grad_gain_ffn: float32 [1536], replicated
- grad_w_gate: float32 [1536, 3968], P(None, 'tensor')
- grad_w_up: float32 [1536, 3968], P(None, 'tensor')
- grad_w_down: float32 [3968, 1536], P('tensor')
Inputs may be any that keep to these rules, and one draw needn't show every extreme that they name: `lengths`: each group's 4 rows fill its 512 tokens exactly; in every group the longest row has 256 tokens.
All inputs are finite; a program needn't handle non-finite values.
Results may differ from a plain program's by a relative error of at most 0.017.
Values may be sent and summed in bfloat16 or wider, within the bound.
No kernel may reach another device: no remote copies, remote signals or barrier semaphores. Data moves between devices by JAX's collectives and lax.ppermute only.
A program may use at most 192 MiB of HBM per device.

v0:
```python
import jax
import jax.numpy as jnp
from jax import lax
from jax.sharding import PartitionSpec as P


def rms_norm(value, gain):
    return value * lax.rsqrt(jnp.mean(value * value, axis=-1, keepdims=True) + 1e-06) * gain


def segment_ids(row_lengths, count):
    ends = jnp.cumsum(row_lengths)
    place = jnp.arange(count, dtype=jnp.int32)
    return jnp.sum((place[:, None] >= ends[None, :-1]).astype(jnp.int32), axis=1)


def inner_product(left, right):
    return lax.dot_general(
        left, right, (((0,), (0,)), ((), ())), preferred_element_type=jnp.float32
    )


def times_transposed(left, right):
    return lax.dot_general(
        left, right, (((1,), (1,)), ((), ())), preferred_element_type=jnp.float32
    )


def skew_rows(series, start, rows, count):
    width = 2 * count
    tiled = jnp.tile(series, (1, rows + 1))
    piece = lax.dynamic_slice_in_dim(tiled, count - 1 - start, rows * (width - 1), 1)
    return piece.reshape(series.shape[0], rows, width - 1)[:, :, :count]


def unskew_rows(grid, start, count):
    heads, rows, _ = grid.shape
    width = 2 * count
    padded = jnp.pad(grid, ((0, 0), (0, 0), (0, width - 1 - count)))
    flat = padded.reshape(heads, rows * (width - 1))
    room = jnp.zeros((heads, (rows + 1) * width), jnp.float32)
    room = lax.dynamic_update_slice_in_dim(room, flat, count - 1 - start, 1)
    return jnp.sum(room.reshape(heads, rows + 1, width), axis=1)


def block_scores(query_block, keys, seg_block, row_id, bias_vec, start, count):
    scores = jnp.einsum("qhd,khd->hqk", query_block, keys, preferred_element_type=jnp.float32)
    scores = scores + skew_rows(bias_vec, start, query_block.shape[0], count)
    same = seg_block[:, None] == row_id[None, :]
    return jnp.where(same[None], scores, -1e30)


def attend_forward(query, keys, values, row_id, bias_vec, block):
    count = query.shape[0]

    def advance(carry, index):
        start = index * block
        scores = block_scores(query, keys, row_id, row_id, bias_vec, start, count)
        highest = jnp.max(scores, axis=2, keepdims=True)
        raised = jnp.exp(scores - highest)
        total = jnp.sum(raised, axis=2, keepdims=True)
        prob_low = (raised / total).astype(jnp.bfloat16)
        result = jnp.einsum("hqk,khd->qhd", prob_low, values, preferred_element_type=jnp.float32)
        return (carry, (result.astype(jnp.bfloat16), (highest + jnp.log(total))[:, :, 0]))

    _, (outputs, logsums) = lax.scan(
        advance, jnp.int32(0), jnp.arange(count // block, dtype=jnp.int32)
    )
    return (outputs.reshape(query.shape), logsums)


def attend_backward(query, keys, values, grad_attn, row_id, bias_vec, logsums, block):
    count, heads, _ = query.shape

    def advance(carry, items):
        grad_keys, grad_values, grad_vec = carry
        index, logsum = items
        start = index * block
        scores = block_scores(query, keys, row_id, row_id, bias_vec, start, count)
        probability = jnp.exp(scores - logsum[:, :, None])
        prob_low = probability.astype(jnp.bfloat16)
        grad_prob = jnp.einsum(
            "qhd,khd->hqk", grad_attn, values, preferred_element_type=jnp.float32
        )
        delta = jnp.sum(probability * grad_prob, axis=2, keepdims=True)
        grad_scores = (probability * (grad_prob - delta)).astype(jnp.bfloat16)
        grad_values = grad_values + jnp.einsum(
            "hqk,qhd->khd", prob_low, grad_attn, preferred_element_type=jnp.float32
        )
        grad_keys = grad_keys + jnp.einsum(
            "hqk,qhd->khd", grad_scores, query, preferred_element_type=jnp.float32
        )
        grad_query = jnp.einsum(
            "hqk,khd->qhd", grad_scores, keys, preferred_element_type=jnp.float32
        )
        grad_vec = grad_vec + unskew_rows(grad_scores.astype(jnp.float32), start, count)
        return ((grad_keys, grad_values, grad_vec), grad_query.astype(jnp.bfloat16))

    zeros = jnp.zeros(query.shape, jnp.float32)
    start_carry = (zeros, zeros, jnp.zeros((heads, 2 * count), jnp.float32))
    (grad_keys, grad_values, grad_vec), grad_query = lax.scan(
        advance, start_carry, (jnp.arange(count // block, dtype=jnp.int32), logsums)
    )
    return (
        grad_query.reshape(query.shape),
        grad_keys.astype(jnp.bfloat16),
        grad_values.astype(jnp.bfloat16),
        grad_vec,
    )


def body(
    tokens,
    cotangent,
    gain_attn,
    w_query,
    w_key,
    w_value,
    w_out,
    bias_table,
    gain_ffn,
    w_gate,
    w_up,
    w_down,
    lengths,
    buckets,
):
    tokens_here = tokens.shape[0]
    count = tokens_here * lax.axis_size("tensor")
    block = min(512, count)
    heads_here = bias_table.shape[1]
    head_size = w_query.shape[1] // heads_here
    bucket_count = bias_table.shape[0]
    row_id = segment_ids(lengths[0], count)
    onehot = (buckets[:, None] == jnp.arange(bucket_count, dtype=jnp.int32)[None, :]).astype(
        jnp.float32
    )
    bias_vec = jnp.dot(onehot, bias_table, precision=lax.Precision.HIGHEST).T
    bias_vec = jnp.pad(bias_vec, ((0, 0), (0, 1)))
    tokens_float = tokens.astype(jnp.float32)
    normed_one = rms_norm(tokens_float, gain_attn).astype(jnp.bfloat16)
    normed_all = lax.all_gather(normed_one, "tensor", axis=0, tiled=True)
    shape = (count, heads_here, head_size)
    query = (
        jnp.dot(normed_all, w_query, preferred_element_type=jnp.float32)
        .astype(jnp.bfloat16)
        .reshape(shape)
    )
    keys = (
        jnp.dot(normed_all, w_key, preferred_element_type=jnp.float32)
        .astype(jnp.bfloat16)
        .reshape(shape)
    )
    values = (
        jnp.dot(normed_all, w_value, preferred_element_type=jnp.float32)
        .astype(jnp.bfloat16)
        .reshape(shape)
    )
    attended, logsums = attend_forward(query, keys, values, row_id, bias_vec, block)
    attn_flat = attended.reshape(count, -1)
    middle = tokens_float + lax.psum_scatter(
        jnp.dot(attn_flat, w_out, preferred_element_type=jnp.float32),
        "tensor",
        scatter_dimension=0,
        tiled=True,
    )
    normed_two = rms_norm(middle, gain_ffn).astype(jnp.bfloat16)
    second_all = lax.all_gather(normed_two, "tensor", axis=0, tiled=True)
    gate = jnp.dot(second_all, w_gate, preferred_element_type=jnp.float32)
    up_value = jnp.dot(second_all, w_up, preferred_element_type=jnp.float32)

    def gated(gate_in, up_in):
        return jax.nn.gelu(gate_in, approximate=True) * up_in

    hidden_value, gated_pull = jax.vjp(gated, gate, up_value)
    hidden = hidden_value.astype(jnp.bfloat16)
    block_out = (
        middle
        + lax.psum_scatter(
            jnp.dot(hidden, w_down, preferred_element_type=jnp.float32).astype(jnp.bfloat16),
            "tensor",
            scatter_dimension=0,
            tiled=True,
        ).astype(jnp.float32)
    ).astype(jnp.bfloat16)
    grad_all = lax.all_gather(cotangent, "tensor", axis=0, tiled=True)
    grad_w_down = inner_product(hidden, grad_all)
    grad_hidden = times_transposed(grad_all, w_down)
    grad_gate_f, grad_up_f = gated_pull(grad_hidden)
    grad_gate = grad_gate_f.astype(jnp.bfloat16)
    grad_up = grad_up_f.astype(jnp.bfloat16)
    grad_w_gate = inner_product(second_all, grad_gate)
    grad_w_up = inner_product(second_all, grad_up)
    left = times_transposed(grad_gate, w_gate)
    grad_normed_two = lax.psum_scatter(
        left + times_transposed(grad_up, w_up), "tensor", scatter_dimension=0, tiled=True
    )
    _, norm_two_pull = jax.vjp(rms_norm, middle, gain_ffn)
    middle_part, grad_gain_ffn = norm_two_pull(grad_normed_two)
    grad_middle = cotangent.astype(jnp.float32) + middle_part
    middle_all = lax.all_gather(grad_middle.astype(jnp.bfloat16), "tensor", axis=0, tiled=True)
    grad_w_out = inner_product(attn_flat, middle_all)
    grad_attn = times_transposed(middle_all, w_out).astype(jnp.bfloat16).reshape(shape)
    grad_query, grad_keys, grad_values, grad_vec = attend_backward(
        query, keys, values, grad_attn, row_id, bias_vec, logsums, block
    )
    grad_table_here = jnp.dot(
        onehot.T, grad_vec[:, : buckets.shape[0]].T, precision=lax.Precision.HIGHEST
    )
    grad_query_flat = grad_query.reshape(count, -1)
    grad_keys_flat = grad_keys.reshape(count, -1)
    grad_values_flat = grad_values.reshape(count, -1)
    grad_w_query = inner_product(normed_all, grad_query_flat)
    grad_w_key = inner_product(normed_all, grad_keys_flat)
    grad_w_value = inner_product(normed_all, grad_values_flat)
    total = times_transposed(grad_query_flat, w_query)
    total = total + times_transposed(grad_keys_flat, w_key)
    grad_normed_one = lax.psum_scatter(
        (total + times_transposed(grad_values_flat, w_value)).astype(jnp.bfloat16),
        "tensor",
        scatter_dimension=0,
        tiled=True,
    ).astype(jnp.float32)
    _, norm_one_pull = jax.vjp(rms_norm, tokens_float, gain_attn)
    input_part, grad_gain_attn = norm_one_pull(grad_normed_one)
    grad_tokens = (grad_middle + input_part).astype(jnp.bfloat16)
    column = lax.axis_index("tensor") * heads_here
    table_wide = jnp.zeros((bucket_count, heads_here * lax.axis_size("tensor")), jnp.float32)
    table_wide = lax.dynamic_update_slice_in_dim(table_wide, grad_table_here, column, 1)
    gain_attn_sum, gain_ffn_sum, table_sum = lax.psum(
        (grad_gain_attn, grad_gain_ffn, table_wide), ("dp", "tensor")
    )
    grad_bias_table = lax.dynamic_slice_in_dim(table_sum, column, heads_here, 1)
    shards = (
        lax.psum_scatter(grad_w_query.reshape(-1), "dp", scatter_dimension=0, tiled=True),
        lax.psum_scatter(grad_w_key.reshape(-1), "dp", scatter_dimension=0, tiled=True),
        lax.psum_scatter(grad_w_value.reshape(-1), "dp", scatter_dimension=0, tiled=True),
        lax.psum_scatter(grad_w_out.reshape(-1), "dp", scatter_dimension=0, tiled=True),
        lax.psum_scatter(grad_w_gate.reshape(-1), "dp", scatter_dimension=0, tiled=True),
        lax.psum_scatter(grad_w_up.reshape(-1), "dp", scatter_dimension=0, tiled=True),
        lax.psum_scatter(grad_w_down.reshape(-1), "dp", scatter_dimension=0, tiled=True),
    )
    summed = (
        lax.all_gather(shards[0].astype(jnp.bfloat16), "dp", axis=0, tiled=True).astype(
            jnp.float32
        ),
        lax.all_gather(shards[1].astype(jnp.bfloat16), "dp", axis=0, tiled=True).astype(
            jnp.float32
        ),
        lax.all_gather(shards[2].astype(jnp.bfloat16), "dp", axis=0, tiled=True).astype(
            jnp.float32
        ),
        lax.all_gather(shards[3].astype(jnp.bfloat16), "dp", axis=0, tiled=True).astype(
            jnp.float32
        ),
        lax.all_gather(shards[4].astype(jnp.bfloat16), "dp", axis=0, tiled=True).astype(
            jnp.float32
        ),
        lax.all_gather(shards[5].astype(jnp.bfloat16), "dp", axis=0, tiled=True).astype(
            jnp.float32
        ),
        lax.all_gather(shards[6].astype(jnp.bfloat16), "dp", axis=0, tiled=True).astype(
            jnp.float32
        ),
    )
    return (
        block_out,
        grad_tokens,
        gain_attn_sum,
        summed[0].reshape(w_query.shape),
        summed[1].reshape(w_key.shape),
        summed[2].reshape(w_value.shape),
        summed[3].reshape(w_out.shape),
        grad_bias_table,
        gain_ffn_sum,
        summed[4].reshape(w_gate.shape),
        summed[5].reshape(w_up.shape),
        summed[6].reshape(w_down.shape),
    )


def solution(mesh):
    placed = (
        P(("dp", "tensor"), None),
        P(("dp", "tensor"), None),
        P(),
        P(None, "tensor"),
        P(None, "tensor"),
        P(None, "tensor"),
        P("tensor", None),
        P(None, "tensor"),
        P(),
        P(None, "tensor"),
        P(None, "tensor"),
        P("tensor", None),
        P("dp", None),
        P(),
    )
    return jax.shard_map(
        body,
        mesh=mesh,
        in_specs=placed,
        out_specs=(
            P(("dp", "tensor"), None),
            P(("dp", "tensor"), None),
            P(),
            P(None, "tensor"),
            P(None, "tensor"),
            P(None, "tensor"),
            P("tensor", None),
            P(None, "tensor"),
            P(),
            P(None, "tensor"),
            P(None, "tensor"),
            P("tensor", None),
        ),
        check_vma=False,
    )
```

profile of v0, /device:TPU:0, one launch (start us, length us, event | category | flops | bytes accessed | tf_op | source)
XLA Modules:
  0.0 1455.3 jit_solution(14522709266037792601)
XLA Ops:
  8.6 1.9 fusion.20
  12.5 7.6 copy.89
  20.1 9.7 dynamic_slice.19
  29.8 13.2 reshape.225
  43.0 3.9 slice.17
  46.9 3.6 copy.87
  51.0 2.4 convolution_convert_fusion.2
  53.3 1.8 convolution_convert_fusion.3
  59.6 2.3 fusion.35
  61.9 40.5 %reduce-scatter.5.cloned.1.call-done = f32[128,1536]{1,0:T(8,128)} async-done(((f32[512,1536]{1,0:T(8,128)}), f32[128,1536]{1,0:T(8,128)}) %reduce-scatter.5.cloned.1.call-update) | async-done | bytes 786448 | tf_op jit(solution)/shard_map/reduce_scatter | solution.py:161
  106.6 18.7 %all-gather.10.cloned.1.call-done = bf16[512,1536]{1,0:T(8,128)(2,1)} async-done(((bf16[128,1536]{1,0:T(8,128)(2,1)}), bf16[512,1536]{1,0:T(8,128)(2,1)}) %all-gather.10.cloned.1.call-update) | async-done | bytes 1572880 | tf_op jit(solution)/shard_map/all_gather | solution.py:168
  125.3 5.5 fusion.37
  130.9 3.1 fusion.36
  133.9 12.5 all-gather.12.cloned.1.call-done
  146.4 6.3 multiply_convert_fusion.1
  152.7 1.8 fusion.38
  155.3 3.6 convolution_add_fusion.2
  158.9 38.0 %reduce-scatter.9.cloned.1.call-done = f32[128,1536]{1,0:T(8,128)} async-done(((f32[512,1536]{1,0:T(8,128)}), f32[128,1536]{1,0:T(8,128)}) %reduce-scatter.9.cloned.1.call-update) | async-done | bytes 786448 | tf_op jit(solution)/shard_map/reduce_scatter | solution.py:195
  196.9 1.7 multiply_reduce_fusion.1
  198.8 2.0 fusion.33
  200.8 19.7 %all-gather.14.cloned.1.call-done = bf16[512,1536]{1,0:T(8,128)(2,1)} async-done(((bf16[128,1536]{1,0:T(8,128)(2,1)}), bf16[512,1536]{1,0:T(8,128)(2,1)}) %all-gather.14.cloned.1.call-update) | async-done | bytes 1572880 | tf_op jit(solution)/shard_map/all_gather | solution.py:201
  220.6 2.2 convolution_convert_fusion.1
  222.8 2.7 fusion.15
  231.0 1.8 fusion
  234.2 4.2 convolution_convert_fusion
  238.5 6.2 fusion.46
  244.6 7.2 reshape.250
  251.8 4.5 fusion.45
  256.3 8.8 reshape.247
  265.2 4.5 fusion.44
  269.6 8.9 reshape.244
  278.5 3.1 fusion.43
  283.0 1.8 fusion.42
  284.8 3.0 reshape.235
  287.8 1.8 fusion.40
  289.6 3.0 reshape.229
  292.6 1.8 fusion.41
  294.4 3.0 reshape.232
  297.4 880.4 %all-reduce.13 = (bf16[294912]{0:T(1024)(128)(2,1)}, bf16[294912]{0:T(1024)(128)(2,1)}, bf16[294912]{0:T(1024)(128)(2,1)}, bf16[294912]{0:T(1024)(128)(2,1)}, bf...) all-reduce(f32[294912]{0:T(1024)} %reshape.229, ...), channel_id=6, replica_groups=mesh['dp'=8,'tensor'=4] {'dp'}, use_global_device_ids=true, to_apply=%region_15.16.clone | all-reduce | flops 5750784 | bytes 34504704
  1177.8 1.9 dynamic-slice.22
  1179.8 1.8 dynamic-slice.23
  1182.3 1.6 copy.88
  1183.8 3.6 pad.13.clone
  1187.4 7.0 reshape.277
  1194.4 5.6 reshape.241
  1200.0 1.8 dynamic-slice.21
  1201.8 8.0 pad_convert_fusion
  1209.8 10.8 reshape.262
  1220.6 3.2 reduce_sum.109
  1227.4 33.0 %all_gather.40 = bf16[294912]{0:T(1024)(128)(2,1)S(1)} all-gather(bf16[36864]{0:T(1024)(128)(2,1)S(1)} %dynamic-slice.24), channel_id=1, replica_groups=mesh['dp'=8,'tensor'=4] {'dp'}, dimensions={0}, use_global_device_ids=true | all-gather | bytes 663552 | tf_op jit(solution)/shard_map/all_gather | solution.py:253
  1260.3 1.6 reshape.260
  1261.9 32.9 %all_gather.37 = bf16[294912]{0:T(1024)(128)(2,1)S(1)} all-gather(bf16[36864]{0:T(1024)(128)(2,1)S(1)} %dynamic-slice.27), channel_id=1, replica_groups=mesh['dp'=8,'tensor'=4] {'dp'}, dimensions={0}, use_global_device_ids=true | all-gather | bytes 663552 | tf_op jit(solution)/shard_map/all_gather | solution.py:244
  1295.2 1.5 copy.73
  1296.7 33.7 %all_gather.38 = bf16[294912]{0:T(1024)(128)(2,1)S(1)} all-gather(bf16[36864]{0:T(1024)(128)(2,1)S(1)} %dynamic-slice.26), channel_id=1, replica_groups=mesh['dp'=8,'tensor'=4] {'dp'}, dimensions={0}, use_global_device_ids=true | all-gather | bytes 663552 | tf_op jit(solution)/shard_map/all_gather | solution.py:247
  1332.2 33.1 %all_gather.39 = bf16[294912]{0:T(1024)(128)(2,1)S(1)} all-gather(bf16[36864]{0:T(1024)(128)(2,1)S(1)} %dynamic-slice.25), channel_id=1, replica_groups=mesh['dp'=8,'tensor'=4] {'dp'}, dimensions={0}, use_global_device_ids=true | all-gather | bytes 663552 | tf_op jit(solution)/shard_map/all_gather | solution.py:250
  1365.4 1.5 reshape.258
  1366.9 3.0 copy.75
  1371.8 37.8 %all-reduce.10 = (f32[1536]{0:T(1024)}, f32[32,12]{0,1:T(8,128)S(1)}, f32[1536]{0:T(1024)}) all-reduce(f32[1536]{0:T(1024)S(1)} %get-tuple-element.110, f32[32,12]{0,1:T(8,128)S(1)} %dynamic_update_slice.16, f32[1536]{0:T(1024)S(1)} %get-tuple-element.108), channel_id=1, replica_groups=mesh['dp'=8,'tensor'=4] {'dp','tensor'}, use_global_device_ids=true, to_apply=%region_14.15 | all-reduce | flops 3456 | bytes 27648 | tf_op jit(solution)/shard_map/psum | solution.py:230
  1410.3 2.4 fusion.24
  1412.7 7.8 reshape.266
  1420.5 6.5 copy.77
  1426.9 7.8 reshape.264
  1434.7 6.5 copy.76
  1441.2 7.1 reshape.268
  (167 shorter events, 29.6 us)
Async XLA Ops:
  7.2 139.2 %copy-start = (bf16[992,1536]{1,0:T(8,128)(2,1)S(1)}, bf16[992,1536]{1,0:T(8,128)(2,1)}, u32[]{:S(2)}) copy-start(bf16[992,1536]{1,0:T(8,128)(2,1)} %param.25) | copy-start | bytes 9142276
  7.2 43.7 %all-gather.8.cloned.1.call-start = ((), (), s32[]{:S(2)}) async-start(), calls=%async_computation.4 | async-start | bytes 1966080 | tf_op jit(solution)/shard_map/all_gather | solution.py:142
  10.5 91.9 %reduce-scatter.5.cloned.1.call-start = ((), (), s32[]{:S(2)}) async-start(), calls=%async_computation.5 | async-start | bytes 3932160 | tf_op jit(solution)/shard_map/reduce_scatter | solution.py:161
  46.9 3.6 copy-start.46
  50.9 2.4 copy-start.9
  51.0 4.2 copy-start.11
  53.3 2.7 copy-start.28
  55.2 0.9 copy-start.30
  56.0 2.2 copy-start.2
  56.0 1.5 copy-start.35
  58.2 0.7 copy-start.37
  58.2 1.4 copy-start.33
  58.9 0.7 copy-start.26
  61.8 40.6 %copy-start.12 = (bf16[128,1536]{1,0:T(8,128)(2,1)S(1)}, bf16[128,1536]{1,0:T(8,128)(2,1)}, u32[]{:S(2)}) copy-start(bf16[128,1536]{1,0:T(8,128)(2,1)} %param.14) | copy-start | bytes 1179652
  61.8 42.8 %copy-start.39 = (f32[1536]{0:T(1024)S(1)}, f32[1536]{0:T(1024)}, u32[]{:S(2)}) copy-start(f32[1536]{0:T(1024)} %param.22) | copy-start | bytes 18436
  61.9 63.4 %all-gather.10.cloned.1.call-start = ((), (), s32[]{:S(2)}) async-start(), calls=%async_computation.6 | async-start | bytes 1966080 | tf_op jit(solution)/shard_map/all_gather | solution.py:168
  103.7 0.9 copy-start.6
  105.5 40.9 %all-gather.12.cloned.1.call-start = ((), (), s32[]{:S(2)}) async-start(), calls=%async_computation.8 | async-start | bytes 1966080 | tf_op jit(solution)/shard_map/all_gather | solution.py:186
  106.1 90.8 %reduce-scatter.9.cloned.1.call-start = ((), (), s32[]{:S(2)}) async-start(), calls=%async_computation.9 | async-start | bytes 3932160 | tf_op jit(solution)/shard_map/reduce_scatter | solution.py:195
  125.3 5.5 copy-start.41
  125.3 5.5 copy-start.43
  146.4 6.3 copy-start.42
  152.7 1.9 copy-start.48
  152.7 1.9 copy-start.24
  152.7 2.6 copy-start.17
  158.9 61.7 %all-gather.14.cloned.1.call-start = ((), (), s32[]{:S(2)}) async-start(), calls=%async_computation.10 | async-start | bytes 1966080 | tf_op jit(solution)/shard_map/all_gather | solution.py:201
  196.9 1.7 copy-start.7
  196.9 1.8 copy-start.13
  200.8 1169.7 %reduce-scatter.11.cloned.1.call-start = ((), (), s32[]{:S(2)}) async-start(), calls=%async_computation.11 | async-start | bytes 1966080 | tf_op jit(solution)/shard_map/reduce_scatter | solution.py:218
  222.8 2.8 copy-start.3
  222.8 2.8 copy-start.38
  225.6 5.0 copy-start.20
  226.3 0.9 copy-start.31
  227.3 2.3 copy-start.4
  227.3 1.1 copy-start.29
  227.3 1.7 copy-start.34
  228.4 1.2 copy-start.18
  228.8 1.8 copy-start.22
  228.8 1.2 copy-start.32
  230.0 1.1 copy-start.36
  231.0 1.9 copy-start.47
  232.9 1177.4 %reduce-scatter.7.cloned.1.call-start = ((), (), s32[]{:S(2)}) async-start(), calls=%async_computation.7 | async-start | bytes 1966080 | tf_op jit(solution)/shard_map/reduce_scatter | solution.py:179
  238.4 1174.3 %all-gather.18.cloned.1.call-start = ((), (), s32[]{:S(2)}) async-start(), calls=%async_computation.13 | async-start | bytes 3428352 | tf_op jit(solution)/shard_map/all_gather | solution.py:259
  244.6 7.2 copy-start.25
  244.6 7.2 copy-start.44
  256.3 8.8 copy-start.49
  269.6 8.9 copy-start.27
  278.5 4.4 copy-start.10
  278.5 4.5 copy-start.21
  284.8 3.0 copy-start.23
  289.6 3.0 copy-start.19
  294.4 3.0 copy-start.15
  1177.8 4.5 copy-start.5
  1179.7 247.2 %all-gather.16.cloned.1.call-start = ((), (), s32[]{:S(2)}) async-start(), calls=%async_computation.12 | async-start | bytes 3428352 | tf_op jit(solution)/shard_map/all_gather | solution.py:256
  1181.6 259.6 %all-gather.20.cloned.1.call-start = ((), (), s32[]{:S(2)}) async-start(), calls=%async_computation.14 | async-start | bytes 3428352 | tf_op jit(solution)/shard_map/all_gather | solution.py:262
  1365.4 4.6 copy-start.45
  1365.4 5.1 copy-start.40
  1366.9 43.4 %copy-start.8 = (f32[128,1536]{1,0:T(8,128)S(1)}, f32[128,1536]{1,0:T(8,128)}, u32[]{:S(2)}) copy-start(f32[128,1536]{1,0:T(8,128)} %copy-done.6) | copy-start | bytes 2359300
  1366.9 43.4 %copy-start.14 = (f32[128,1536]{1,0:T(8,128)S(1)}, f32[128,1536]{1,0:T(8,128)}, u32[]{:S(2)}) copy-start(f32[128,1536]{1,0:T(8,128)} %reduce-scatter.9.cloned.1.call-done) | copy-start | bytes 2359300
  1366.9 43.4 %copy-start.16 = (bf16[128,1536]{1,0:T(8,128)(2,1)S(1)}, bf16[128,1536]{1,0:T(8,128)(2,1)}, u32[]{:S(2)}) copy-start(bf16[128,1536]{1,0:T(8,128)(2,1)} %param.15) | copy-start | bytes 1179652
  1441.2 7.1 copy-start.1
Sparse Core Ops, SparseCore 0:
  10.6 22.3 all-gather.7
  62.0 40.3 reduce-scatter.4
  105.6 19.6 all-gather.9
  126.7 19.6 all-gather.11
  159.0 37.8 reduce-scatter.8
  200.9 19.6 all-gather.13
  233.0 27.9 reduce-scatter.10
  263.5 28.0 reduce-scatter.6
  1179.8 58.6 all-gather.17
  1241.1 68.7 all-gather.15
  1312.1 63.6 all-gather.19
where the time goes:
time: 1460 us
  blocking collectives  1050 us (72%)
  local copies, waits for them, and re-layouts  164 us (11%)
  waiting for transfers between devices  130 us (9%)
  matrix products  67.8 us (5%)
  other arithmetic  25.8 us (2%)
  between operations  16.2 us (1%)
    unnamed x1, blocking collectives  880 us
    unnamed x118, local copies, waits for them, and re-layouts  54.3 us
    reduce_scatter x1, waiting for transfers between devices, body(): lax.psum_scatter(jnp.dot(attn_flat, w_out, preferred_element_type=jnp.flo...  40.5 us
    reduce_scatter x1, waiting for transfers between devices, body(): lax.psum_scatter(left + times_transposed(grad_up, w_up), 'tensor', scatte...  38 us
    psum x1, blocking collectives, body(): lax.psum((grad_gain_attn, grad_gain_ffn, table_wide), ('dp', 'tensor'))  37.8 us
    all_gather x1, blocking collectives, body(): lax.all_gather(shards[1].astype(jnp.bfloat16), 'dp', axis=0, tiled=True)  33.7 us
    all_gather x1, blocking collectives, body(): lax.all_gather(shards[2].astype(jnp.bfloat16), 'dp', axis=0, tiled=True)  33.1 us
    all_gather x1, blocking collectives, body(): lax.all_gather(shards[3].astype(jnp.bfloat16), 'dp', axis=0, tiled=True)  33 us
  transfers between devices with their start and end apart: 11, of which 5 were waited for; matrix products, arithmetic and copies ran while one was open for 14% of the time, Pallas kernels for 0%

commit v1 on v0

v1 whole, which is shorter than its diff:
```python
import functools

import jax
import jax.numpy as jnp
from jax import lax
from jax.experimental import pallas as pl
from jax.experimental.pallas import tpu as pltpu
from jax.sharding import PartitionSpec as P

F32 = jnp.float32
BF16 = jnp.bfloat16
ORDER = (0, 2, 1, 3)


def swap_bits(index):
    return ((index & 1) << 1) | (index >> 1)


def dot_nn(left, right):
    return lax.dot_general(left, right, (((1,), (0,)), ((), ())), preferred_element_type=F32)


def dot_tn(left, right):
    return lax.dot_general(left, right, (((0,), (0,)), ((), ())), preferred_element_type=F32)


def dot_nt(left, right):
    return lax.dot_general(left, right, (((1,), (1,)), ((), ())), preferred_element_type=F32)


def attn_forward_kernel(
    place_ref, lens_ref, table_ref, buckets_ref, qkv_ref, attn_ref, prob_ref, tiles_ref, *, heads, size, blk, nblk
):
    step = pl.program_id(0)
    place = place_ref[0]
    inner = heads * size

    @pl.when(step == 0)
    def _():
        buckets = buckets_ref[...]
        for h in range(heads):
            vec = jnp.zeros(buckets.shape, F32)
            for b in range(table_ref.shape[0]):
                vec = jnp.where(buckets == b, table_ref[b, h], vec)
            for d in range(2 * nblk - 1):
                seg = jnp.broadcast_to(vec[:, d * blk : (d + 2) * blk], (blk, 2 * blk))
                tiles_ref[h, d] = pltpu.roll(seg, blk, 1, stride=1, stride_axis=0)[:, :blk]

    def row_of(pos):
        row, end = jnp.zeros(pos.shape, jnp.int32), jnp.int32(0)
        for r in range(lens_ref.shape[1] - 1):
            end = end + lens_ref[0, r]
            row = row + (pos >= end).astype(jnp.int32)
        return row

    here = place ^ swap_bits(step)
    row_q = row_of(here * blk + lax.broadcasted_iota(jnp.int32, (blk, 1), 0))
    lane = lax.broadcasted_iota(jnp.int32, (1, blk), 1)
    row_k = jnp.concatenate([row_of((place ^ m) * blk + lane) for m in ORDER], axis=1)
    same = row_q == row_k
    rows = pl.ds(step * blk, blk)
    for h in range(heads):
        query = qkv_ref[rows, h * size : (h + 1) * size]
        keys = qkv_ref[:, inner + h * size : inner + (h + 1) * size]
        values = qkv_ref[:, 2 * inner + h * size : 2 * inner + (h + 1) * size]
        bias = jnp.concatenate([tiles_ref[h, (place ^ m) - here + nblk - 1] for m in ORDER], axis=1)
        scores = jnp.where(same, dot_nt(query, keys) + bias, -1e30)
        raised = jnp.exp(scores - jnp.max(scores, axis=1, keepdims=True))
        prob = (raised * (1.0 / jnp.sum(raised, axis=1, keepdims=True))).astype(BF16)
        prob_ref[h] = prob
        attn_ref[:, h * size : (h + 1) * size] = dot_nn(prob, values).astype(BF16)


def attn_forward(place, lens, table, buckets, qkv, heads, size, blk):
    count = qkv.shape[0]
    nblk = count // blk
    return pl.pallas_call(
        functools.partial(attn_forward_kernel, heads=heads, size=size, blk=blk, nblk=nblk),
        out_shape=(
            jax.ShapeDtypeStruct((count, heads * size), BF16),
            jax.ShapeDtypeStruct((heads, count, count), BF16),
        ),
        grid_spec=pltpu.PrefetchScalarGridSpec(
            num_scalar_prefetch=3,
            grid=(nblk,),
            in_specs=[
                pl.BlockSpec(buckets.shape, lambda i, *_: (0, 0)),
                pl.BlockSpec(qkv.shape, lambda i, *_: (0, 0)),
            ],
            out_specs=[
                pl.BlockSpec((blk, heads * size), lambda i, *_: (i, 0)),
                pl.BlockSpec((heads, blk, count), lambda i, *_: (0, i, 0)),
            ],
            scratch_shapes=[pltpu.VMEM((heads, 2 * nblk - 1, blk, blk), F32)],
        ),
        cost_estimate=pl.CostEstimate(flops=8 * heads * count * count * size, bytes_accessed=4 * heads * count * count, transcendentals=heads * count * count),
        name="attn_forward",
    )(place, lens, table, buckets, qkv)


def attn_backward_kernel(
    place_ref, buckets_ref, qkv_ref, grad_ref, prob_ref, gqkv_ref, gtable_ref, dk_ref, dv_ref, tiles_ref, vec_ref,
    *, heads, size, blk, nblk, bins
):
    step = pl.program_id(0)
    place = place_ref[0]
    inner = heads * size

    @pl.when(step == 0)
    def _():
        dk_ref[...] = jnp.zeros_like(dk_ref)
        dv_ref[...] = jnp.zeros_like(dv_ref)
        tiles_ref[...] = jnp.zeros_like(tiles_ref)

    here = place ^ swap_bits(step)
    rows = pl.ds(step * blk, blk)
    for h in range(heads):
        query = qkv_ref[rows, h * size : (h + 1) * size]
        keys = qkv_ref[:, inner + h * size : inner + (h + 1) * size]
        values = qkv_ref[:, 2 * inner + h * size : 2 * inner + (h + 1) * size]
        grad = grad_ref[rows, h * size : (h + 1) * size]
        prob_low = prob_ref[h]
        prob = prob_low.astype(F32)
        grad_prob = dot_nt(grad, values)
        delta = jnp.sum(prob * grad_prob, axis=1, keepdims=True)
        grad_scores = (prob * (grad_prob - delta)).astype(BF16)
        dv_ref[h] += dot_tn(prob_low, grad)
        dk_ref[h] += dot_tn(grad_scores, query)
        gqkv_ref[rows, h * size : (h + 1) * size] = dot_nn(grad_scores, keys).astype(BF16)
        for b, m in enumerate(ORDER):
            tiles_ref[h, (place ^ m) - here + nblk - 1] += grad_scores[:, b * blk : (b + 1) * blk].astype(F32)

    @pl.when(step == nblk - 1)
    def _():
        vec_ref[...] = jnp.zeros_like(vec_ref)
        back = (
            lax.broadcasted_iota(jnp.int32, (blk, blk), 0) + lax.broadcasted_iota(jnp.int32, (blk, blk), 1) == blk - 1
        ).astype(F32)
        for h in range(heads):
            gqkv_ref[:, inner + h * size : inner + (h + 1) * size] = dk_ref[h].astype(BF16)
            gqkv_ref[:, 2 * inner + h * size : 2 * inner + (h + 1) * size] = dv_ref[h].astype(BF16)
            for d in range(2 * nblk - 1):
                flip = jnp.dot(back, tiles_ref[h, d], precision=lax.Precision.HIGHEST, preferred_element_type=F32)
                wide = jnp.concatenate([flip, jnp.zeros((blk, blk), F32)], axis=1)
                moved = pltpu.roll(wide, 1, 1, stride=1, stride_axis=0)
                vec_ref[h : h + 1, d * blk : (d + 2) * blk] += jnp.sum(moved, axis=0, keepdims=True)
        pick = (lax.broadcasted_iota(jnp.int32, (bins, 1), 0) == buckets_ref[...]).astype(F32)
        gtable_ref[...] = lax.dot_general(
            pick, vec_ref[...], (((1,), (1,)), ((), ())), precision=lax.Precision.HIGHEST, preferred_element_type=F32
        )


def attn_backward(place, buckets, qkv, grad, prob, heads, size, blk, bins):
    count = qkv.shape[0]
    nblk = count // blk
    whole = lambda i, *_: (0, 0)
    return pl.pallas_call(
        functools.partial(attn_backward_kernel, heads=heads, size=size, blk=blk, nblk=nblk, bins=bins),
        out_shape=(jax.ShapeDtypeStruct(qkv.shape, BF16), jax.ShapeDtypeStruct((bins, 8), F32)),
        grid_spec=pltpu.PrefetchScalarGridSpec(
            num_scalar_prefetch=1,
            grid=(nblk,),
            in_specs=[
                pl.BlockSpec(buckets.shape, whole),
                pl.BlockSpec(qkv.shape, whole),
                pl.BlockSpec(grad.shape, whole),
                pl.BlockSpec((heads, blk, count), lambda i, *_: (0, i, 0)),
            ],
            out_specs=[pl.BlockSpec(qkv.shape, whole), pl.BlockSpec((bins, 8), whole)],
            scratch_shapes=[
                pltpu.VMEM((heads, count, size), F32),
                pltpu.VMEM((heads, count, size), F32),
                pltpu.VMEM((heads, 2 * nblk - 1, blk, blk), F32),
                pltpu.VMEM((8, 2 * nblk * blk), F32),
            ],
        ),
        cost_estimate=pl.CostEstimate(flops=10 * heads * count * count * size, bytes_accessed=4 * heads * count * count, transcendentals=0),
        name="attn_backward",
    )(place, buckets, qkv, grad, prob)


def after(value, *gates):
    return lax.optimization_barrier((value, *gates))[0]


def body(
    tokens, cotangent, gain_attn, w_query, w_key, w_value, w_out, bias_table, gain_ffn, w_gate, w_up, w_down, lengths, buckets,
):
    n_t, n_d = lax.axis_size("tensor"), lax.axis_size("dp")
    blk, width = tokens.shape
    heads = bias_table.shape[1]
    inner = w_query.shape[1]
    size = inner // heads
    bins = bias_table.shape[0]
    t_at, d_at = lax.axis_index("tensor"), lax.axis_index("dp")
    x_at, z_at, n_z = d_at & 1, d_at >> 1, n_d // 2

    def tensor_swap(value, mask):
        return lax.ppermute(value, "tensor", [(i, i ^ mask) for i in range(n_t)])

    def dp_swap(value, mask):
        return lax.ppermute(value, "dp", [(i, i ^ mask) for i in range(n_d)])

    def z_send(value, pairs):
        return lax.ppermute(value, "dp", [(2 * a + x, 2 * b + x) for a, b in pairs for x in (0, 1)])

    def z_sum(value):
        if n_z == 4:
            value = value + z_send(value, ((0, 1), (3, 2)))
            value = value + z_send(value, ((1, 2), (2, 1)))
            ends = z_send(value, ((1, 0), (2, 3)))
            return jnp.where((z_at == 0) | (z_at == 3), ends, value)
        step = 2
        while step < n_d:
            value = value + dp_swap(value, step)
            step *= 2
        return value

    def in_order(mine, other):
        first = x_at == 0
        return jnp.where(first, mine, other), jnp.where(first, other, mine)

    tok_y = tensor_swap(tokens, 2)
    tok_c = tensor_swap(tokens, 1)
    tok_yc = tensor_swap(tok_y, 1)
    tok_all = jnp.concatenate([tokens, tok_y, tok_c, tok_yc], axis=0).astype(F32)
    rr1_all = lax.rsqrt(jnp.mean(tok_all * tok_all, axis=1, keepdims=True) + 1e-6)
    n1 = (tok_all * rr1_all * gain_attn).astype(BF16)

    w_qkv = jnp.concatenate([w_query, w_key, w_value], axis=1)
    qkv = dot_nn(n1, w_qkv).astype(BF16)

    wo_own = after(w_out, tok_y)
    wo_y = tensor_swap(wo_own, 2)
    wo_c = tensor_swap(wo_own, 1)
    wo_yc = tensor_swap(wo_y, 1)
    wo_all = jnp.concatenate([w_out, wo_y, wo_c, wo_yc], axis=0)

    def gather8(value):
        from_y = tensor_swap(value, 2)
        from_x = dp_swap(value, 1)
        half = blk // 2
        diag = jnp.concatenate([tensor_swap(from_x[:half], 2), dp_swap(from_y[half:], 1)], axis=0)
        near = jnp.concatenate([value, from_x, from_y, diag], axis=0)
        return jnp.concatenate([near, tensor_swap(near, 1)], axis=0)

    def scatter8(near, far):
        near = near + tensor_swap(far, 1)
        near = near[: 2 * blk] + tensor_swap(near[2 * blk :], 2)
        return near[:blk].astype(F32) + dp_swap(near[blk:], 1).astype(F32)

    def scatter4(near, far):
        near = near + tensor_swap(far, 1)
        return near[:blk].astype(F32) + tensor_swap(near[blk:], 2).astype(F32)

    cot_all = gather8(after(cotangent, tok_y))

    place = t_at.astype(jnp.int32).reshape(1)
    bucket_row = jnp.pad(buckets, (1, 0), constant_values=-1).reshape(1, -1)
    attn, prob = attn_forward(place, lengths, bias_table, bucket_row, qkv, heads, size, blk)

    def to_owners(blocks):
        return [blocks[0]] + [tensor_swap(blocks[b], ORDER[b]) for b in range(1, n_t)]

    mine = to_owners([attn[b * blk : (b + 1) * blk] for b in range(n_t)])
    tok = tokens.astype(F32)
    y1 = tok + dot_nn(jnp.concatenate(mine, axis=1), wo_all)
    rr2 = lax.rsqrt(jnp.mean(y1 * y1, axis=1, keepdims=True) + 1e-6)
    n2 = (y1 * rr2 * gain_ffn).astype(BF16)
    n2_all = gather8(n2)

    units = w_down.shape[0]
    half = -(-units // 256) * 128
    spare = 2 * half - units
    wg = lax.dynamic_slice_in_dim(jnp.pad(w_gate, ((0, 0), (0, spare))), x_at * half, half, 1)
    wu = lax.dynamic_slice_in_dim(jnp.pad(w_up, ((0, 0), (0, spare))), x_at * half, half, 1)
    wd = lax.dynamic_slice_in_dim(jnp.pad(w_down, ((0, spare), (0, 0))), x_at * half, half, 0)

    grad_hidden = dot_nt(cot_all, wd)
    gate = dot_nn(n2_all, wg)
    up = dot_nn(n2_all, wu)

    def gated(g, u):
        return jax.nn.gelu(g, approximate=True) * u

    hidden_f, pull = jax.vjp(gated, gate, up)
    hidden = hidden_f.astype(BF16)
    gg_f, gu_f = pull(grad_hidden)
    gg, gu = gg_f.astype(BF16), gu_f.astype(BF16)

    def spread(value, parts):
        rows = value.shape[0] // parts
        done = [z_sum(value[i * rows : (i + 1) * rows]) for i in range(parts)]
        both = [in_order(piece, dp_swap(piece, 1)) for piece in done]
        return [b[0] for b in both], [b[1] for b in both]

    down_a, down_b = spread(dot_tn(hidden, cot_all).astype(BF16), 2)
    out_w_down = jnp.concatenate(down_a + down_b, axis=0)[:units].astype(F32)
    gate_a, gate_b = spread(dot_tn(n2_all, gg).astype(BF16), 2)
    out_w_gate = jnp.concatenate([jnp.concatenate(gate_a, 0), jnp.concatenate(gate_b, 0)[:, : units - half]], 1).astype(F32)
    up_a, up_b = spread(dot_tn(n2_all, gu).astype(BF16), 2)
    out_w_up = jnp.concatenate([jnp.concatenate(up_a, 0), jnp.concatenate(up_b, 0)[:, : units - half]], 1).astype(F32)

    side = n_t * blk
    gn2_part = (dot_nt(gg, wg) + dot_nt(gu, wu)).astype(BF16)
    gn2 = scatter8(gn2_part[:side], gn2_part[side:])
    ffn_part = dot_nn(hidden, wd).astype(BF16)
    block_out = (y1 + scatter8(ffn_part[:side], ffn_part[side:])).astype(BF16)

    gain2_part = jnp.sum(gn2 * y1 * rr2, axis=0)
    c2 = gn2 * gain_ffn
    gy1 = cotangent.astype(F32) + rr2 * c2 - y1 * (rr2 * rr2 * rr2) * jnp.mean(c2 * y1, axis=1, keepdims=True)
    gy1_low = gy1.astype(BF16)
    ga_mine = dot_nt(gy1_low, wo_all).astype(BF16)
    ga = jnp.concatenate(to_owners([ga_mine[:, b * inner : (b + 1) * inner] for b in range(n_t)]), axis=0)

    gqkv, gtable = attn_backward(place, bucket_row, qkv, ga, prob, heads, size, blk, bins)

    gy_own = after(gy1_low, ga)
    gy_y = tensor_swap(gy_own, 2)
    gy_near = jnp.concatenate([gy_own, gy_y], axis=0)
    gy_all = jnp.concatenate([gy_near, tensor_swap(gy_near, 1)], axis=0)

    def full_sum(value):
        rows = value.shape[0] // 2
        give = lax.dynamic_slice_in_dim(value, (1 - x_at) * rows, rows, 0)
        keep = lax.dynamic_slice_in_dim(value, x_at * rows, rows, 0)
        piece = z_sum(keep + dp_swap(give, 1))
        return jnp.concatenate(in_order(piece, dp_swap(piece, 1)), axis=0)

    out_w_out = full_sum(dot_tn(attn, gy_all).astype(BF16)).astype(F32)
    g_wqkv = full_sum(dot_tn(n1, gqkv).astype(BF16)).astype(F32)
    gn1_part = dot_nt(gqkv, w_qkv).astype(BF16)
    gn1 = scatter4(gn1_part[: 2 * blk], gn1_part[2 * blk :])

    rr1 = lax.rsqrt(jnp.mean(tok * tok, axis=1, keepdims=True) + 1e-6)
    gain1_part = jnp.sum(gn1 * tok * rr1, axis=0)
    c1 = gn1 * gain_attn
    grad_tokens = (gy1 + rr1 * c1 - tok * (rr1 * rr1 * rr1) * jnp.mean(c1 * tok, axis=1, keepdims=True)).astype(BF16)

    small = jnp.concatenate([gain1_part, gain2_part])
    step = 1
    while step < n_t:
        small = small + tensor_swap(small, step)
        step *= 2
    small = jnp.concatenate([small, gtable.reshape(-1)])
    step = 1
    while step < n_d:
        small = small + dp_swap(small, step)
        step *= 2
    gain1_sum, gain2_sum = small[:width], small[width : 2 * width]
    table_sum = small[2 * width :].reshape(gtable.shape)[:, :heads]

    return (
        block_out,
        grad_tokens,
        gain1_sum,
        g_wqkv[:, :inner],
        g_wqkv[:, inner : 2 * inner],
        g_wqkv[:, 2 * inner :],
        out_w_out,
        table_sum,
        gain2_sum,
        out_w_gate,
        out_w_up,
        out_w_down,
    )


def solution(mesh):
    rows, cols, both = P("tensor", None), P(None, "tensor"), P(("dp", "tensor"), None)
    return jax.shard_map(
        body,
        mesh=mesh,
        in_specs=(both, both, P(), cols, cols, cols, rows, cols, P(), cols, cols, rows, P("dp", None), P()),
        out_specs=(both, both, P(), cols, cols, cols, rows, cols, P(), cols, cols, rows),
        check_vma=False,
    )
```

time: 1460 us -> 578 us (0.40)
  blocking collectives: 1050 us -> 0 us
  waiting for transfers between devices: 130 us -> 314 us
  local copies, waits for them, and re-layouts: 164 us -> 49.1 us
  starting transfers between devices: 0.92 us -> 86.5 us
  other arithmetic: 25.8 us -> 70.3 us
  matrix products: 67.8 us -> 29.1 us
  Pallas kernels: 0 us -> 18.3 us
    unnamed x1 -> x0, blocking collectives: 880 us -> none
    ppermute x0 -> x71, waiting for transfers between devices: none -> 314 us  [the longest x24 191 us: z_send(): lax.ppermute(value, 'dp', [(2 * a + x, 2 * b + x) for a, b in pairs for x...]
    all_gather x4 -> x0, blocking collectives: 133 us -> none  [the longest x1 33.7 us: body(): lax.all_gather(shards[1].astype(jnp.bfloat16), 'dp', axis=0, tiled=True)]
    reshape x17 -> x1, local copies, waits for them, and re-layouts: 91.5 us -> 1.41 us  [body(): small = jnp.concatenate([small, gtable.reshape(-1)])]
    ppermute x0 -> x71, starting transfers between devices: none -> 86.5 us  [the longest x24 41.4 us: z_send(): lax.ppermute(value, 'dp', [(2 * a + x, 2 * b + x) for a, b in pairs for x...]
    reduce_scatter x4 -> x0, waiting for transfers between devices: 78.5 us -> none  [the longest x1 40.5 us: body(): lax.psum_scatter(jnp.dot(attn_flat, w_out, preferred_element_type=jnp.flo...]
    all_gather x7 -> x0, waiting for transfers between devices: 50.9 us -> none  [the longest x1 19.7 us: body(): lax.all_gather(grad_middle.astype(jnp.bfloat16), 'tensor', axis=0, tiled=...]
    dot_general x29 -> x15, matrix products: 67.8 us -> 29.1 us  [the longest x5 9.99 us: dot_tn(): lax.dot_general(left, right, (((0,), (0,)), ((), ())), preferred_element_...]
  transfers between devices with their start and end apart: 11 -> 71, of which waited for: 5 -> 27; matrix products, arithmetic and copies ran while one was open for 14% -> 22% of each run, Pallas kernels for 0% -> 3%
where the time goes in v1:
time: 578 us; the launch traced here: 570 us
  waiting for transfers between devices  314 us (54%)
  starting transfers between devices  86.5 us (15%)
  other arithmetic  70.3 us (12%)
  local copies, waits for them, and re-layouts  49.1 us (8%)
  matrix products  29.1 us (5%)
  Pallas kernels  18.3 us (3%)
    ppermute x24, waiting for transfers between devices, z_send(): lax.ppermute(value, 'dp', [(2 * a + x, 2 * b + x) for a, b in pairs for x...  191 us
    ppermute x19, waiting for transfers between devices, dp_swap(): return lax.ppermute(value, 'dp', [(i, i ^ mask) for i in range(n_d)])  94.1 us
    ppermute x24, starting transfers between devices, z_send(): lax.ppermute(value, 'dp', [(2 * a + x, 2 * b + x) for a, b in pairs for x...  41.4 us
    unnamed x123, local copies, waits for them, and re-layouts  31.9 us
    ppermute x28, waiting for transfers between devices, tensor_swap(): return lax.ppermute(value, 'tensor', [(i, i ^ mask) for i in range(n_t)])  28.8 us
    ppermute x19, starting transfers between devices, dp_swap(): return lax.ppermute(value, 'dp', [(i, i ^ mask) for i in range(n_d)])  24.4 us
    ppermute x28, starting transfers between devices, tensor_swap(): return lax.ppermute(value, 'tensor', [(i, i ^ mask) for i in range(n_t)])  20.7 us
    convert_element_type x1, other arithmetic, body(): jnp.concatenate([jnp.concatenate(up_a, 0), jnp.concatenate(up_b, 0)[:, :u...  13.6 us
  transfers between devices with their start and end apart: 71, of which 27 were waited for; matrix products, arithmetic and copies ran while one was open for 22% of the time, Pallas kernels for 3%

profile of v1, /device:TPU:0, one launch (start us, length us, event | category | flops | bytes accessed | tf_op | source)
XLA Modules:
  0.0 569.9 jit_solution(17328457043857118866)
XLA Ops:
  0.6 3.1 collective-permute-start
  9.9 3.2 collective-permute-done
  13.2 1.8 collective-permute-start.6
  18.2 1.6 fusion
  19.8 3.5 convolution_convert_fusion.7.qkv_ref
  23.3 8.5 %attn_forward.1 = (bf16[512,192]{1,0:T(8,128)(2,1)}, bf16[3,512,512]{2,1,0:T(8,128)(2,1)}) custom-call(s32[1]{0:T(128)} %bitcast.place_ref, s32[1,4]{1,0:T(1,128)} %lens_ref.1, f32[32,3]{1,0:T(8,128)} %copy.31.table_ref, s32[1,1024]{1,0:T(1,128)} %bitcast.24, bf16[512,576]{1,0:T(8,128)(2,1)} %convolution_convert_fusion.7.qkv_ref), custom_call_target="tpu_custom_call" | custom-call | flops 402653184 | bytes 3145728 | tf_op jit(solution)/shard_map/attn_forward/pallas_call | solution.py:77
  35.5 1.9 constant_dynamic-update-slice_fusion.21
  38.1 1.7 collective-permute-start.19
  41.1 3.8 collective-permute-done.19
  46.8 1.7 collective-permute-start.20
  52.1 1.6 collective-permute-start.10
  55.0 8.0 %collective-permute-done.9 = bf16[128,1536]{1,0:T(8,128)(2,1)S(1)} collective-permute-done((bf16[128,1536]{1,0:T(8,128)(2,1)S(1)}, bf16[128,1536]{1,0:T(8,128)(2,1)S(1)}, u32[]{:S(2)}, u32[]{:S(2)}) %collective-permute-start.9) | collective-permute-done | bytes 393248 | tf_op jit(solution)/shard_map/ppermute | solution.py:202
  63.0 1.6 collective-permute-start.11
  67.5 1.7 collective-permute-done.11
  71.3 1.7 copy-done.34
  72.9 2.8 constant_dynamic-update-slice_fusion.23
  78.2 1.8 fusion.21
  80.1 1.8 fusion.22
  82.9 3.8 multiply_convert_fusion
  86.7 1.8 fusion.20
  88.5 1.9 convolution_convert_fusion.4
  90.3 1.9 convolution_convert_fusion.3
  92.2 1.8 add_convert_fusion
  94.7 3.5 collective-permute-start.47
  102.4 1.8 convolution_convert_fusion.2
  104.4 11.7 %collective-permute-done.47 = bf16[768,512]{1,0:T(8,128)(2,1)S(1)} collective-permute-done((bf16[768,512]{1,0:T(8,128)(2,1)S(1)}, bf16[768,512]{1,0:T(8,128)(2,1)S(1)}, u32[]{:S(2)}, u32[]{:S(2)}) %collective-permute-start.47) | collective-permute-done | bytes 786464 | tf_op jit(solution)/shard_map/ppermute | solution.py:205
  116.1 4.4 collective-permute-start.63
  120.5 12.4 %collective-permute-done.51 = bf16[768,512]{1,0:T(8,128)(2,1)S(1)} collective-permute-done((bf16[768,512]{1,0:T(8,128)(2,1)S(1)}, bf16[768,512]{1,0:T(8,128)(2,1)S(1)}, u32[]{:S(2)}, u32[]{:S(2)}) %collective-permute-start.51) | collective-permute-done | bytes 786464 | tf_op jit(solution)/shard_map/ppermute | solution.py:205
  133.0 4.4 collective-permute-start.67
  137.4 1.8 convolution_convert_fusion
  139.3 10.5 %collective-permute-done.55 = bf16[768,512]{1,0:T(8,128)(2,1)S(1)} collective-permute-done((bf16[768,512]{1,0:T(8,128)(2,1)S(1)}, bf16[768,512]{1,0:T(8,128)(2,1)S(1)}, u32[]{:S(2)}, u32[]{:S(2)}) %collective-permute-start.55) | collective-permute-done | bytes 786464 | tf_op jit(solution)/shard_map/ppermute | solution.py:205
  150.0 16.6 %collective-permute-done.59 = bf16[768,512]{1,0:T(8,128)(2,1)S(1)} collective-permute-done((bf16[768,512]{1,0:T(8,128)(2,1)S(1)}, bf16[768,512]{1,0:T(8,128)(2,1)S(1)}, u32[]{:S(2)}, u32[]{:S(2)}) %collective-permute-start.59) | collective-permute-done | bytes 786464 | tf_op jit(solution)/shard_map/ppermute | solution.py:205
  168.4 15.1 %collective-permute-done.63 = bf16[256,1536]{1,0:T(8,128)(2,1)S(1)} collective-permute-done((bf16[256,1536]{1,0:T(8,128)(2,1)S(1)}, bf16[256,1536]{1,0:T(8,128)(2,1)S(1)}, u32[]{:S(2)}, u32[]{:S(2)}) %collective-permute-start.63) | collective-permute-done | bytes 786464 | tf_op jit(solution)/shard_map/ppermute | solution.py:205
  184.2 15.3 %collective-permute-done.67 = bf16[256,1536]{1,0:T(8,128)(2,1)S(1)} collective-permute-done((bf16[256,1536]{1,0:T(8,128)(2,1)S(1)}, bf16[256,1536]{1,0:T(8,128)(2,1)S(1)}, u32[]{:S(2)}, u32[]{:S(2)}) %collective-permute-start.67) | collective-permute-done | bytes 786464 | tf_op jit(solution)/shard_map/ppermute | solution.py:205
  204.4 1.6 collective-permute-start.68
  206.0 1.7 collective-permute-start.64
  213.2 1.7 add.211
  216.7 1.6 add.213
  219.7 1.6 add.219
  222.7 1.6 add.217
  224.3 4.2 collective-permute-done.23
  231.0 12.6 %collective-permute-done.15 = bf16[256,1536]{1,0:T(8,128)(2,1)} collective-permute-done((bf16[256,1536]{1,0:T(8,128)(2,1)}, bf16[256,1536]{1,0:T(8,128)(2,1)}, u32[]{:S(2)}, u32[]{:S(2)}) %collective-permute-start.15) | collective-permute-done | bytes 786464 | tf_op jit(solution)/shard_map/ppermute | solution.py:199
  246.2 63.5 %collective-permute-done.69 = bf16[256,1536]{1,0:T(8,128)(2,1)S(1)} collective-permute-done((bf16[256,1536]{1,0:T(8,128)(2,1)S(1)}, bf16[256,1536]{1,0:T(8,128)(2,1)S(1)}, u32[]{:S(2)}, u32[]{:S(2)}) %collective-permute-start.69) | collective-permute-done | bytes 786464 | tf_op jit(solution)/shard_map/ppermute | solution.py:205
  314.4 26.7 %collective-permute-done.65 = bf16[256,1536]{1,0:T(8,128)(2,1)S(1)} collective-permute-done((bf16[256,1536]{1,0:T(8,128)(2,1)S(1)}, bf16[256,1536]{1,0:T(8,128)(2,1)S(1)}, u32[]{:S(2)}, u32[]{:S(2)}) %collective-permute-start.65) | collective-permute-done | bytes 786464 | tf_op jit(solution)/shard_map/ppermute | solution.py:205
  347.9 5.2 collective-permute-done.16
  363.8 9.8 %attn_backward.1 = (bf16[512,576]{1,0:T(8,128)(2,1)}, f32[32,8]{1,0:T(8,128)}) custom-call(s32[1]{0:T(128)} %bitcast.place_ref, s32[1,1024]{1,0:T(1,128)} %bitcast.25, bf16[512,576]{1,0:T(8,128)(2,1)} %convolution_convert_fusion.7.qkv_ref, bf16[512,192]{1,0:T(8,128)(2,1)} %pad_maximum_fusion.7.grad_ref, bf16[3,512,512]{2,1,0:T(8,128)(2,1)} %get-tuple-element.22.prob_ref), custom_call_target="tpu_custom_call" | custom-call | flops 503316480 | bytes 3145728 | tf_op jit(solution)/shard_map/attn_backward/pallas_call | solution.py:157
  373.6 3.9 convolution_convert_fusion.1
  381.6 39.0 %collective-permute-done.70 = bf16[256,1536]{1,0:T(8,128)(2,1)} collective-permute-done((bf16[256,1536]{1,0:T(8,128)(2,1)}, bf16[256,1536]{1,0:T(8,128)(2,1)}, u32[]{:S(2)}, u32[]{:S(2)}) %collective-permute-start.70) | collective-permute-done | bytes 786464 | tf_op jit(solution)/shard_map/ppermute | solution.py:202
  423.6 13.9 %collective-permute-done.66 = bf16[256,1536]{1,0:T(8,128)(2,1)} collective-permute-done((bf16[256,1536]{1,0:T(8,128)(2,1)}, bf16[256,1536]{1,0:T(8,128)(2,1)}, u32[]{:S(2)}, u32[]{:S(2)}) %collective-permute-start.66) | collective-permute-done | bytes 786464 | tf_op jit(solution)/shard_map/ppermute | solution.py:202
  444.5 13.5 %fusion.6 = f32[1536,992]{1,0:T(8,128)} fusion(bf16[768,512]{1,0:T(8,128)(2,1)S(1)} %get-tuple-element.85, bf16[768,512]{1,0:T(8,128)(2,1)S(1)} %get-tuple-element.83, bf16[768,512]{1,0:T(8,128)(2,1)S(1)} %get-tuple-element.84, bf16[768,512]{1,0:T(8,128)(2,1)S(1)} %get-tuple-element.82), kind=kLoop, calls=%fused_computation.12 | loop fusion | flops 12189696 | bytes 9240576 | tf_op jit(solution)/shard_map/convert_element_type | solution.py:300
  458.1 1.6 broadcast_select_fusion.15
  461.5 8.6 %collective-permute-done.35 = bf16[768,576]{0,1:T(8,128)(2,1)S(1)} collective-permute-done((bf16[768,576]{0,1:T(8,128)(2,1)S(1)}, bf16[768,576]{0,1:T(8,128)(2,1)S(1)}, u32[]{:S(2)}, u32[]{:S(2)}) %collective-permute-start.35) | collective-permute-done | bytes 884768 | tf_op jit(solution)/shard_map/ppermute | solution.py:202
  475.8 13.6 %fusion.4 = f32[1536,992]{1,0:T(8,128)} fusion(bf16[768,512]{1,0:T(8,128)(2,1)S(1)} %get-tuple-element.77, bf16[768,512]{1,0:T(8,128)(2,1)S(1)} %get-tuple-element.75, bf16[768,512]{1,0:T(8,128)(2,1)S(1)} %get-tuple-element.76, bf16[768,512]{1,0:T(8,128)(2,1)S(1)} %get-tuple-element.74), kind=kLoop, calls=%fused_computation.9 | loop fusion | flops 12189696 | bytes 9240576 | tf_op jit(solution)/shard_map/convert_element_type | solution.py:302
  490.8 1.6 collective-permute-start.37
  492.5 3.6 collective-permute-start.43
  496.1 2.9 fusion.7
  499.0 6.5 %copy.33 = f32[1536,992]{0,1:T(8,128)} copy(f32[1536,992]{1,0:T(8,128)} %fusion.6) | data formatting | bytes 12189696
  505.4 6.5 %copy.34 = f32[1536,992]{0,1:T(8,128)} copy(f32[1536,992]{1,0:T(8,128)} %fusion.4) | data formatting | bytes 12189696
  514.6 2.7 collective-permute-done.33
  517.3 2.1 collective-permute-start.34
  526.1 6.2 %collective-permute-done.45 = bf16[96,1536]{1,0:T(8,128)(2,1)} collective-permute-done((bf16[96,1536]{1,0:T(8,128)(2,1)}, bf16[96,1536]{1,0:T(8,128)(2,1)}, u32[]{:S(2)}, u32[]{:S(2)}) %collective-permute-start.45) | collective-permute-done | bytes 294944 | tf_op jit(solution)/shard_map/ppermute | solution.py:205
  534.8 13.3 %collective-permute-done.38 = bf16[768,576]{0,1:T(8,128)(2,1)S(1)} collective-permute-done((bf16[768,576]{0,1:T(8,128)(2,1)S(1)}, bf16[768,576]{0,1:T(8,128)(2,1)S(1)}, u32[]{:S(2)}, u32[]{:S(2)}) %collective-permute-start.38) | collective-permute-done | bytes 884768 | tf_op jit(solution)/shard_map/ppermute | solution.py:205
  551.3 15.7 %collective-permute-done.39 = bf16[768,576]{0,1:T(8,128)(2,1)S(1)} collective-permute-done((bf16[768,576]{0,1:T(8,128)(2,1)S(1)}, bf16[768,576]{0,1:T(8,128)(2,1)S(1)}, u32[]{:S(2)}, u32[]{:S(2)}) %collective-permute-start.39) | collective-permute-done | bytes 884768 | tf_op jit(solution)/shard_map/ppermute | solution.py:202
  567.6 1.9 fusion.58
  (311 shorter events, 118.2 us)
Async XLA Ops:
  0.6 12.5 %collective-permute-start = (bf16[128,1536]{1,0:T(8,128)(2,1)}, bf16[128,1536]{1,0:T(8,128)(2,1)}, u32[]{:S(2)}, u32[]{:S(2)}) collective-permute-start(bf16[128,1536]{1,0:T(8,128)(2,1)} %param.14), channel_id=1, source_target_pairs={{0,2},{1,3},{2,0},{3,1},{4,6},{5,7},{6,4},{7,5},{8,10},{9,11},{10,... | collective-permute-start | bytes 1179656 | tf_op jit(solution)/shard_map/ppermute | solution.py:199
  3.7 13.9 %collective-permute-start.1 = (bf16[128,1536]{1,0:T(8,128)(2,1)}, bf16[128,1536]{1,0:T(8,128)(2,1)}, u32[]{:S(2)}, u32[]{:S(2)}) collective-permute-start(bf16[128,1536]{1,0:T(8,128)(2,1)} %param.14), channel_id=1, source_target_pairs={{0,1},{1,0},{2,3},{3,2},{4,5},{5,4},{6,7},{7,6},{8,9},{9,8},{10,11... | collective-permute-start | bytes 1179656 | tf_op jit(solution)/shard_map/ppermute | solution.py:199
  13.2 27.6 %collective-permute-start.6 = (bf16[192,1536]{1,0:T(8,128)(2,1)}, bf16[192,1536]{1,0:T(8,128)(2,1)}, u32[]{:S(2)}, u32[]{:S(2)}) collective-permute-start(bf16[192,1536]{1,0:T(8,128)(2,1)} %param.20), channel_id=1, source_target_pairs={{0,2},{1,3},{2,0},{3,1},{4,6},{5,7},{6,4},{7,5},{8,10},{9,11},{10,... | collective-permute-start | bytes 1769480 | tf_op jit(solution)/shard_map/ppermute | solution.py:199
  15.0 31.8 %collective-permute-start.7 = (bf16[192,1536]{1,0:T(8,128)(2,1)}, bf16[192,1536]{1,0:T(8,128)(2,1)}, u32[]{:S(2)}, u32[]{:S(2)}) collective-permute-start(bf16[192,1536]{1,0:T(8,128)(2,1)} %param.20), channel_id=1, source_target_pairs={{0,1},{1,0},{2,3},{3,2},{4,5},{5,4},{6,7},{7,6},{8,9},{9,8},{10,11... | collective-permute-start | bytes 1769480 | tf_op jit(solution)/shard_map/ppermute | solution.py:199
  15.2 18.5 %collective-permute-start.17 = (bf16[128,1536]{1,0:T(8,128)(2,1)S(1)}, bf16[128,1536]{1,0:T(8,128)(2,1)}, u32[]{:S(2)}, u32[]{:S(2)}) collective-permute-start(bf16[128,1536]{1,0:T(8,128)(2,1)S(1)} %copy-done.16), channel_id=1, source_target_pairs={{0,4},{4,0},{8,12},{12,8},{16,20},{20,16},{24,28},{28,24},{1,5},{5... | collective-permute-start | bytes 1179656 | tf_op jit(solution)/shard_map/ppermute | solution.py:202
  17.7 20.4 %collective-permute-start.18 = (bf16[128,1536]{1,0:T(8,128)(2,1)S(1)}, bf16[128,1536]{1,0:T(8,128)(2,1)S(1)}, u32[]{:S(2)}, u32[]{:S(2)}) collective-permute-start(bf16[128,1536]{1,0:T(8,128)(2,1)S(1)} %copy-done.16), channel_id=1, source_target_pairs={{0,2},{1,3},{2,0},{3,1},{4,6},{5,7},{6,4},{7,5},{8,10},{9,11},{10,... | collective-permute-start | bytes 1179656 | tf_op jit(solution)/shard_map/ppermute | solution.py:199
  32.8 16.8 %collective-permute-start.5 = (bf16[128,192]{1,0:T(8,128)(2,1)S(1)}, bf16[128,192]{1,0:T(8,128)(2,1)S(1)}, u32[]{:S(2)}, u32[]{:S(2)}) collective-permute-start(bf16[128,192]{1,0:T(8,128)(2,1)S(1)} %get-tuple-element.104), channel_id=1, source_target_pairs={{0,3},{1,2},{2,1},{3,0},{4,7},{5,6},{6,5},{7,4},{8,11},{9,10},{10,... | collective-permute-start | bytes 147464 | tf_op jit(solution)/shard_map/ppermute | solution.py:199
  33.7 15.9 %collective-permute-start.4 = (bf16[128,192]{1,0:T(8,128)(2,1)S(1)}, bf16[128,192]{1,0:T(8,128)(2,1)S(1)}, u32[]{:S(2)}, u32[]{:S(2)}) collective-permute-start(bf16[128,192]{1,0:T(8,128)(2,1)S(1)} %get-tuple-element.105), channel_id=1, source_target_pairs={{0,1},{1,0},{2,3},{3,2},{4,5},{5,4},{6,7},{7,6},{8,9},{9,8},{10,11... | collective-permute-start | bytes 147464 | tf_op jit(solution)/shard_map/ppermute | solution.py:199
  38.1 6.8 %collective-permute-start.19 = (bf16[64,1536]{1,0:T(8,128)(2,1)S(1)}, bf16[64,1536]{1,0:T(8,128)(2,1)S(1)}, u32[]{:S(2)}, u32[]{:S(2)}) collective-permute-start(bf16[64,1536]{1,0:T(8,128)(2,1)S(1)} %slice.195), channel_id=1, source_target_pairs={{0,2},{1,3},{2,0},{3,1},{4,6},{5,7},{6,4},{7,5},{8,10},{9,11},{10,... | collective-permute-start | bytes 589832 | tf_op jit(solution)/shard_map/ppermute | solution.py:199
  40.8 8.9 %collective-permute-start.3 = (bf16[128,192]{1,0:T(8,128)(2,1)S(1)}, bf16[128,192]{1,0:T(8,128)(2,1)S(1)}, u32[]{:S(2)}, u32[]{:S(2)}) collective-permute-start(bf16[128,192]{1,0:T(8,128)(2,1)S(1)} %get-tuple-element.106), channel_id=1, source_target_pairs={{0,2},{1,3},{2,0},{3,1},{4,6},{5,7},{6,4},{7,5},{8,10},{9,11},{10,... | collective-permute-start | bytes 147464 | tf_op jit(solution)/shard_map/ppermute | solution.py:199
  46.8 7.4 %collective-permute-start.20 = (bf16[64,1536]{1,0:T(8,128)(2,1)S(1)}, bf16[64,1536]{1,0:T(8,128)(2,1)S(1)}, u32[]{:S(2)}, u32[]{:S(2)}) collective-permute-start(bf16[64,1536]{1,0:T(8,128)(2,1)S(1)} %slice.196), channel_id=1, source_target_pairs={{0,4},{4,0},{8,12},{12,8},{16,20},{20,16},{24,28},{28,24},{1,5},{5... | collective-permute-start | bytes 589832 | tf_op jit(solution)/shard_map/ppermute | solution.py:202
  51.7 11.2 %collective-permute-start.9 = (bf16[128,1536]{1,0:T(8,128)(2,1)S(1)}, bf16[128,1536]{1,0:T(8,128)(2,1)S(1)}, u32[]{:S(2)}, u32[]{:S(2)}) collective-permute-start(bf16[128,1536]{1,0:T(8,128)(2,1)S(1)} %get-tuple-element.57), channel_id=1, source_target_pairs={{0,4},{4,0},{8,12},{12,8},{16,20},{20,16},{24,28},{28,24},{1,5},{5... | collective-permute-start | bytes 1179656 | tf_op jit(solution)/shard_map/ppermute | solution.py:202
  52.1 12.4 %collective-permute-start.10 = (bf16[128,1536]{1,0:T(8,128)(2,1)S(1)}, bf16[128,1536]{1,0:T(8,128)(2,1)S(1)}, u32[]{:S(2)}, u32[]{:S(2)}) collective-permute-start(bf16[128,1536]{1,0:T(8,128)(2,1)S(1)} %get-tuple-element.57), channel_id=1, source_target_pairs={{0,2},{1,3},{2,0},{3,1},{4,6},{5,7},{6,4},{7,5},{8,10},{9,11},{10,... | collective-permute-start | bytes 1179656 | tf_op jit(solution)/shard_map/ppermute | solution.py:199
  54.9 18.0 %collective-permute-start.21 = (bf16[512,1536]{1,0:T(8,128)(2,1)}, bf16[512,1536]{1,0:T(8,128)(2,1)}, u32[]{:S(2)}, u32[]{:S(2)}) collective-permute-start(bf16[512,1536]{1,0:T(8,128)(2,1)} %get-tuple-element.111), channel_id=1, source_target_pairs={{0,1},{1,0},{2,3},{3,2},{4,5},{5,4},{6,7},{7,6},{8,9},{9,8},{10,11... | collective-permute-start | bytes 4718600 | tf_op jit(solution)/shard_map/ppermute | solution.py:199
  63.0 6.2 %collective-permute-start.11 = (bf16[64,1536]{1,0:T(8,128)(2,1)S(1)}, bf16[64,1536]{1,0:T(8,128)(2,1)S(1)}, u32[]{:S(2)}, u32[]{:S(2)}) collective-permute-start(bf16[64,1536]{1,0:T(8,128)(2,1)S(1)} %slice.187), channel_id=1, source_target_pairs={{0,2},{1,3},{2,0},{3,1},{4,6},{5,7},{6,4},{7,5},{8,10},{9,11},{10,... | collective-permute-start | bytes 589832 | tf_op jit(solution)/shard_map/ppermute | solution.py:199
  64.6 6.0 %collective-permute-start.12 = (bf16[64,1536]{1,0:T(8,128)(2,1)S(1)}, bf16[64,1536]{1,0:T(8,128)(2,1)S(1)}, u32[]{:S(2)}, u32[]{:S(2)}) collective-permute-start(bf16[64,1536]{1,0:T(8,128)(2,1)S(1)} %slice.188), channel_id=1, source_target_pairs={{0,4},{4,0},{8,12},{12,8},{16,20},{20,16},{24,28},{28,24},{1,5},{5... | collective-permute-start | bytes 589832 | tf_op jit(solution)/shard_map/ppermute | solution.py:202
  94.1 107.5 %collective-permute-start.22 = (bf16[512,1536]{1,0:T(8,128)(2,1)S(1)}, bf16[512,1536]{1,0:T(8,128)(2,1)S(1)}, u32[]{:S(2)}, u32[]{:S(2)}) collective-permute-start(bf16[512,1536]{1,0:T(8,128)(2,1)S(1)} %slice.198), channel_id=1, source_target_pairs={{0,1},{1,0},{2,3},{3,2},{4,5},{5,4},{6,7},{7,6},{8,9},{9,8},{10,11... | collective-permute-start | bytes 4718600 | tf_op jit(solution)/shard_map/ppermute | solution.py:199
  94.7 21.4 %collective-permute-start.47 = (bf16[768,512]{1,0:T(8,128)(2,1)S(1)}, bf16[768,512]{1,0:T(8,128)(2,1)S(1)}, u32[]{:S(2)}, u32[]{:S(2)}) collective-permute-start(bf16[768,512]{1,0:T(8,128)(2,1)S(1)} %get-tuple-element.88), channel_id=1, source_target_pairs={{0,8},{4,12},{24,16},{28,20},{1,9},{5,13},{25,17},{29,21},{2,10},{... | collective-permute-start | bytes 2359304 | tf_op jit(solution)/shard_map/ppermute | solution.py:205
  98.3 34.7 %collective-permute-start.51 = (bf16[768,512]{1,0:T(8,128)(2,1)S(1)}, bf16[768,512]{1,0:T(8,128)(2,1)S(1)}, u32[]{:S(2)}, u32[]{:S(2)}) collective-permute-start(bf16[768,512]{1,0:T(8,128)(2,1)S(1)} %get-tuple-element.89), channel_id=1, source_target_pairs={{0,8},{4,12},{24,16},{28,20},{1,9},{5,13},{25,17},{29,21},{2,10},{... | collective-permute-start | bytes 2359304 | tf_op jit(solution)/shard_map/ppermute | solution.py:205
  99.7 50.1 %collective-permute-start.55 = (bf16[768,512]{1,0:T(8,128)(2,1)S(1)}, bf16[768,512]{1,0:T(8,128)(2,1)S(1)}, u32[]{:S(2)}, u32[]{:S(2)}) collective-permute-start(bf16[768,512]{1,0:T(8,128)(2,1)S(1)} %get-tuple-element.80), channel_id=1, source_target_pairs={{0,8},{4,12},{24,16},{28,20},{1,9},{5,13},{25,17},{29,21},{2,10},{... | collective-permute-start | bytes 2359304 | tf_op jit(solution)/shard_map/ppermute | solution.py:205
  101.1 65.6 %collective-permute-start.59 = (bf16[768,512]{1,0:T(8,128)(2,1)S(1)}, bf16[768,512]{1,0:T(8,128)(2,1)S(1)}, u32[]{:S(2)}, u32[]{:S(2)}) collective-permute-start(bf16[768,512]{1,0:T(8,128)(2,1)S(1)} %get-tuple-element.81), channel_id=1, source_target_pairs={{0,8},{4,12},{24,16},{28,20},{1,9},{5,13},{25,17},{29,21},{2,10},{... | collective-permute-start | bytes 2359304 | tf_op jit(solution)/shard_map/ppermute | solution.py:205
  116.1 67.4 %collective-permute-start.63 = (bf16[256,1536]{1,0:T(8,128)(2,1)S(1)}, bf16[256,1536]{1,0:T(8,128)(2,1)S(1)}, u32[]{:S(2)}, u32[]{:S(2)}) collective-permute-start(bf16[256,1536]{1,0:T(8,128)(2,1)S(1)} %get-tuple-element.72), channel_id=1, source_target_pairs={{0,8},{4,12},{24,16},{28,20},{1,9},{5,13},{25,17},{29,21},{2,10},{... | collective-permute-start | bytes 2359304 | tf_op jit(solution)/shard_map/ppermute | solution.py:205
  133.0 66.5 %collective-permute-start.67 = (bf16[256,1536]{1,0:T(8,128)(2,1)S(1)}, bf16[256,1536]{1,0:T(8,128)(2,1)S(1)}, u32[]{:S(2)}, u32[]{:S(2)}) collective-permute-start(bf16[256,1536]{1,0:T(8,128)(2,1)S(1)} %get-tuple-element.73), channel_id=1, source_target_pairs={{0,8},{4,12},{24,16},{28,20},{1,9},{5,13},{25,17},{29,21},{2,10},{... | collective-permute-start | bytes 2359304 | tf_op jit(solution)/shard_map/ppermute | solution.py:205
  149.8 54.6 %collective-permute-start.14 = (bf16[512,1536]{1,0:T(8,128)(2,1)S(1)}, bf16[512,1536]{1,0:T(8,128)(2,1)S(1)}, u32[]{:S(2)}, u32[]{:S(2)}) collective-permute-start(bf16[512,1536]{1,0:T(8,128)(2,1)S(1)} %slice.190), channel_id=1, source_target_pairs={{0,1},{1,0},{2,3},{3,2},{4,5},{5,4},{6,7},{7,6},{8,9},{9,8},{10,11... | collective-permute-start | bytes 4718600 | tf_op jit(solution)/shard_map/ppermute | solution.py:199
  166.7 39.3 %collective-permute-start.52 = (bf16[768,512]{1,0:T(8,128)(2,1)S(1)}, bf16[768,512]{1,0:T(8,128)(2,1)S(1)}, u32[]{:S(2)}, u32[]{:S(2)}) collective-permute-start(bf16[768,512]{1,0:T(8,128)(2,1)S(1)} %get-tuple-element.87), channel_id=1, source_target_pairs={{8,16},{12,20},{16,8},{20,12},{9,17},{13,21},{17,9},{21,13},{10,18... | collective-permute-start | bytes 2359304 | tf_op jit(solution)/shard_map/ppermute | solution.py:205
  183.5 24.2 %collective-permute-start.48 = (bf16[768,512]{1,0:T(8,128)(2,1)S(1)}, bf16[768,512]{1,0:T(8,128)(2,1)S(1)}, u32[]{:S(2)}, u32[]{:S(2)}) collective-permute-start(bf16[768,512]{1,0:T(8,128)(2,1)S(1)} %get-tuple-element.86), channel_id=1, source_target_pairs={{8,16},{12,20},{16,8},{20,12},{9,17},{13,21},{17,9},{21,13},{10,18... | collective-permute-start | bytes 2359304 | tf_op jit(solution)/shard_map/ppermute | solution.py:205
  199.5 10.9 %collective-permute-start.60 = (bf16[768,512]{1,0:T(8,128)(2,1)S(1)}, bf16[768,512]{1,0:T(8,128)(2,1)S(1)}, u32[]{:S(2)}, u32[]{:S(2)}) collective-permute-start(bf16[768,512]{1,0:T(8,128)(2,1)S(1)} %get-tuple-element.79), channel_id=1, source_target_pairs={{8,16},{12,20},{16,8},{20,12},{9,17},{13,21},{17,9},{21,13},{10,18... | collective-permute-start | bytes 2359304 | tf_op jit(solution)/shard_map/ppermute | solution.py:205
  201.6 13.7 %collective-permute-start.56 = (bf16[768,512]{1,0:T(8,128)(2,1)}, bf16[768,512]{1,0:T(8,128)(2,1)}, u32[]{:S(2)}, u32[]{:S(2)}) collective-permute-start(bf16[768,512]{1,0:T(8,128)(2,1)} %get-tuple-element.78), channel_id=1, source_target_pairs={{8,16},{12,20},{16,8},{20,12},{9,17},{13,21},{17,9},{21,13},{10,18... | collective-permute-start | bytes 2359304 | tf_op jit(solution)/shard_map/ppermute | solution.py:205
  204.4 13.9 %collective-permute-start.68 = (bf16[256,1536]{1,0:T(8,128)(2,1)}, bf16[256,1536]{1,0:T(8,128)(2,1)}, u32[]{:S(2)}, u32[]{:S(2)}) collective-permute-start(bf16[256,1536]{1,0:T(8,128)(2,1)} %get-tuple-element.71), channel_id=1, source_target_pairs={{8,16},{12,20},{16,8},{20,12},{9,17},{13,21},{17,9},{21,13},{10,18... | collective-permute-start | bytes 2359304 | tf_op jit(solution)/shard_map/ppermute | solution.py:205
  206.0 15.3 %collective-permute-start.64 = (bf16[256,1536]{1,0:T(8,128)(2,1)}, bf16[256,1536]{1,0:T(8,128)(2,1)}, u32[]{:S(2)}, u32[]{:S(2)}) collective-permute-start(bf16[256,1536]{1,0:T(8,128)(2,1)} %get-tuple-element.70), channel_id=1, source_target_pairs={{8,16},{12,20},{16,8},{20,12},{9,17},{13,21},{17,9},{21,13},{10,18... | collective-permute-start | bytes 2359304 | tf_op jit(solution)/shard_map/ppermute | solution.py:205
  207.7 20.8 %collective-permute-start.23 = (bf16[256,1536]{1,0:T(8,128)(2,1)}, bf16[256,1536]{1,0:T(8,128)(2,1)}, u32[]{:S(2)}, u32[]{:S(2)}) collective-permute-start(bf16[256,1536]{1,0:T(8,128)(2,1)} %slice.200), channel_id=1, source_target_pairs={{0,2},{1,3},{2,0},{3,1},{4,6},{5,7},{6,4},{7,5},{8,10},{9,11},{10,... | collective-permute-start | bytes 2359304 | tf_op jit(solution)/shard_map/ppermute | solution.py:199
  211.3 32.4 %collective-permute-start.15 = (bf16[256,1536]{1,0:T(8,128)(2,1)}, bf16[256,1536]{1,0:T(8,128)(2,1)}, u32[]{:S(2)}, u32[]{:S(2)}) collective-permute-start(bf16[256,1536]{1,0:T(8,128)(2,1)} %slice.192), channel_id=1, source_target_pairs={{0,2},{1,3},{2,0},{3,1},{4,6},{5,7},{6,4},{7,5},{8,10},{9,11},{10,... | collective-permute-start | bytes 2359304 | tf_op jit(solution)/shard_map/ppermute | solution.py:199
  215.4 96.6 %collective-permute-start.53 = (bf16[768,512]{1,0:T(8,128)(2,1)S(1)}, bf16[768,512]{1,0:T(8,128)(2,1)S(1)}, u32[]{:S(2)}, u32[]{:S(2)}) collective-permute-start(bf16[768,512]{1,0:T(8,128)(2,1)S(1)} %add.211), channel_id=1, source_target_pairs={{8,0},{12,4},{16,24},{20,28},{9,1},{13,5},{17,25},{21,29},{10,2},{... | collective-permute-start | bytes 2359304 | tf_op jit(solution)/shard_map/ppermute | solution.py:205
  218.3 125.4 %collective-permute-start.49 = (bf16[768,512]{1,0:T(8,128)(2,1)S(1)}, bf16[768,512]{1,0:T(8,128)(2,1)S(1)}, u32[]{:S(2)}, u32[]{:S(2)}) collective-permute-start(bf16[768,512]{1,0:T(8,128)(2,1)S(1)} %add.209), channel_id=1, source_target_pairs={{8,0},{12,4},{16,24},{20,28},{9,1},{13,5},{17,25},{21,29},{10,2},{... | collective-permute-start | bytes 2359304 | tf_op jit(solution)/shard_map/ppermute | solution.py:205
  221.3 123.9 %collective-permute-start.61 = (bf16[768,512]{1,0:T(8,128)(2,1)S(1)}, bf16[768,512]{1,0:T(8,128)(2,1)S(1)}, u32[]{:S(2)}, u32[]{:S(2)}) collective-permute-start(bf16[768,512]{1,0:T(8,128)(2,1)S(1)} %add.215), channel_id=1, source_target_pairs={{8,0},{12,4},{16,24},{20,28},{9,1},{13,5},{17,25},{21,29},{10,2},{... | collective-permute-start | bytes 2359304 | tf_op jit(solution)/shard_map/ppermute | solution.py:205
  228.5 81.2 %collective-permute-start.69 = (bf16[256,1536]{1,0:T(8,128)(2,1)S(1)}, bf16[256,1536]{1,0:T(8,128)(2,1)S(1)}, u32[]{:S(2)}, u32[]{:S(2)}) collective-permute-start(bf16[256,1536]{1,0:T(8,128)(2,1)S(1)} %add.219), channel_id=1, source_target_pairs={{8,0},{12,4},{16,24},{20,28},{9,1},{13,5},{17,25},{21,29},{10,2},{... | collective-permute-start | bytes 2359304 | tf_op jit(solution)/shard_map/ppermute | solution.py:205
  243.7 113.0 %collective-permute-start.57 = (bf16[768,512]{1,0:T(8,128)(2,1)S(1)}, bf16[768,512]{1,0:T(8,128)(2,1)S(1)}, u32[]{:S(2)}, u32[]{:S(2)}) collective-permute-start(bf16[768,512]{1,0:T(8,128)(2,1)S(1)} %add.213), channel_id=1, source_target_pairs={{8,0},{12,4},{16,24},{20,28},{9,1},{13,5},{17,25},{21,29},{10,2},{... | collective-permute-start | bytes 2359304 | tf_op jit(solution)/shard_map/ppermute | solution.py:205
  309.7 31.4 %collective-permute-start.65 = (bf16[256,1536]{1,0:T(8,128)(2,1)S(1)}, bf16[256,1536]{1,0:T(8,128)(2,1)S(1)}, u32[]{:S(2)}, u32[]{:S(2)}) collective-permute-start(bf16[256,1536]{1,0:T(8,128)(2,1)S(1)} %add.217), channel_id=1, source_target_pairs={{8,0},{12,4},{16,24},{20,28},{9,1},{13,5},{17,25},{21,29},{10,2},{... | collective-permute-start | bytes 2359304 | tf_op jit(solution)/shard_map/ppermute | solution.py:205
  312.0 35.6 %collective-permute-start.24 = (bf16[128,1536]{1,0:T(8,128)(2,1)S(1)}, bf16[128,1536]{1,0:T(8,128)(2,1)S(1)}, u32[]{:S(2)}, u32[]{:S(2)}) collective-permute-start(bf16[128,1536]{1,0:T(8,128)(2,1)S(1)} %slice.202), channel_id=1, source_target_pairs={{0,4},{4,0},{8,12},{12,8},{16,20},{20,16},{24,28},{28,24},{1,5},{5... | collective-permute-start | bytes 1179656 | tf_op jit(solution)/shard_map/ppermute | solution.py:202
  341.1 12.0 %collective-permute-start.16 = (bf16[128,1536]{1,0:T(8,128)(2,1)S(1)}, bf16[128,1536]{1,0:T(8,128)(2,1)S(1)}, u32[]{:S(2)}, u32[]{:S(2)}) collective-permute-start(bf16[128,1536]{1,0:T(8,128)(2,1)S(1)} %slice.194), channel_id=1, source_target_pairs={{0,4},{4,0},{8,12},{12,8},{16,20},{20,16},{24,28},{28,24},{1,5},{5... | collective-permute-start | bytes 1179656 | tf_op jit(solution)/shard_map/ppermute | solution.py:202
  343.6 95.4 %collective-permute-start.54 = (bf16[768,512]{1,0:T(8,128)(2,1)}, bf16[768,512]{1,0:T(8,128)(2,1)}, u32[]{:S(2)}, u32[]{:S(2)}) collective-permute-start(bf16[768,512]{1,0:T(8,128)(2,1)} %broadcast_select_fusion.11), channel_id=1, source_target_pairs={{0,4},{4,0},{8,12},{12,8},{16,20},{20,16},{24,28},{28,24},{1,5},{5... | collective-permute-start | bytes 2359304 | tf_op jit(solution)/shard_map/ppermute | solution.py:202
  345.2 96.9 %collective-permute-start.50 = (bf16[768,512]{1,0:T(8,128)(2,1)}, bf16[768,512]{1,0:T(8,128)(2,1)}, u32[]{:S(2)}, u32[]{:S(2)}) collective-permute-start(bf16[768,512]{1,0:T(8,128)(2,1)} %broadcast_select_fusion.12), channel_id=1, source_target_pairs={{0,4},{4,0},{8,12},{12,8},{16,20},{20,16},{24,28},{28,24},{1,5},{5... | collective-permute-start | bytes 2359304 | tf_op jit(solution)/shard_map/ppermute | solution.py:202
  355.6 5.3 collective-permute-start.26
  359.5 98.6 %collective-permute-start.62 = (bf16[768,512]{1,0:T(8,128)(2,1)}, bf16[768,512]{1,0:T(8,128)(2,1)}, u32[]{:S(2)}, u32[]{:S(2)}) collective-permute-start(bf16[768,512]{1,0:T(8,128)(2,1)} %broadcast_select_fusion.9), channel_id=1, source_target_pairs={{0,4},{4,0},{8,12},{12,8},{16,20},{20,16},{24,28},{28,24},{1,5},{5... | collective-permute-start | bytes 2359304 | tf_op jit(solution)/shard_map/ppermute | solution.py:202
  361.0 59.7 %collective-permute-start.70 = (bf16[256,1536]{1,0:T(8,128)(2,1)}, bf16[256,1536]{1,0:T(8,128)(2,1)}, u32[]{:S(2)}, u32[]{:S(2)}) collective-permute-start(bf16[256,1536]{1,0:T(8,128)(2,1)} %broadcast_select_fusion.3), channel_id=1, source_target_pairs={{0,4},{4,0},{8,12},{12,8},{16,20},{20,16},{24,28},{28,24},{1,5},{5... | collective-permute-start | bytes 2359304 | tf_op jit(solution)/shard_map/ppermute | solution.py:202
  361.5 76.0 %collective-permute-start.66 = (bf16[256,1536]{1,0:T(8,128)(2,1)}, bf16[256,1536]{1,0:T(8,128)(2,1)}, u32[]{:S(2)}, u32[]{:S(2)}) collective-permute-start(bf16[256,1536]{1,0:T(8,128)(2,1)} %broadcast_select_fusion.4), channel_id=1, source_target_pairs={{0,4},{4,0},{8,12},{12,8},{16,20},{20,16},{24,28},{28,24},{1,5},{5... | collective-permute-start | bytes 2359304 | tf_op jit(solution)/shard_map/ppermute | solution.py:202
  420.6 40.6 %collective-permute-start.58 = (bf16[768,512]{1,0:T(8,128)(2,1)S(1)}, bf16[768,512]{1,0:T(8,128)(2,1)S(1)}, u32[]{:S(2)}, u32[]{:S(2)}) collective-permute-start(bf16[768,512]{1,0:T(8,128)(2,1)S(1)} %broadcast_select_fusion.10), channel_id=1, source_target_pairs={{0,4},{4,0},{8,12},{12,8},{16,20},{20,16},{24,28},{28,24},{1,5},{5... | collective-permute-start | bytes 2359304 | tf_op jit(solution)/shard_map/ppermute | solution.py:202
  437.5 22.3 %collective-permute-start.28 = (bf16[256,1536]{1,0:T(8,128)(2,1)S(1)}, bf16[256,1536]{1,0:T(8,128)(2,1)S(1)}, u32[]{:S(2)}, u32[]{:S(2)}) collective-permute-start(bf16[256,1536]{1,0:T(8,128)(2,1)S(1)} %slice.208), channel_id=1, source_target_pairs={{0,1},{1,0},{2,3},{3,2},{4,5},{5,4},{6,7},{7,6},{8,9},{9,8},{10,11... | collective-permute-start | bytes 2359304 | tf_op jit(solution)/shard_map/ppermute | solution.py:199
  439.0 31.0 %collective-permute-start.35 = (bf16[768,576]{0,1:T(8,128)(2,1)S(1)}, bf16[768,576]{0,1:T(8,128)(2,1)S(1)}, u32[]{:S(2)}, u32[]{:S(2)}) collective-permute-start(bf16[768,576]{0,1:T(8,128)(2,1)S(1)} %constant_dynamic-slice_fusion.1), channel_id=1, source_target_pairs={{0,4},{4,0},{8,12},{12,8},{16,20},{20,16},{24,28},{28,24},{1,5},{5... | collective-permute-start | bytes 2654216 | tf_op jit(solution)/shard_map/ppermute | solution.py:202
  442.0 17.6 %collective-permute-start.40 = (bf16[128,1536]{1,0:T(8,128)(2,1)S(1)}, bf16[128,1536]{1,0:T(8,128)(2,1)S(1)}, u32[]{:S(2)}, u32[]{:S(2)}) collective-permute-start(bf16[128,1536]{1,0:T(8,128)(2,1)S(1)} %copy-done.6), channel_id=1, source_target_pairs={{0,2},{1,3},{2,0},{3,1},{4,6},{5,7},{6,4},{7,5},{8,10},{9,11},{10,... | collective-permute-start | bytes 1179656 | tf_op jit(solution)/shard_map/ppermute | solution.py:199
  459.7 12.9 %collective-permute-start.41 = (bf16[256,1536]{1,0:T(8,128)(2,1)S(1)}, bf16[256,1536]{1,0:T(8,128)(2,1)S(1)}, u32[]{:S(2)}, u32[]{:S(2)}) collective-permute-start(bf16[256,1536]{1,0:T(8,128)(2,1)S(1)} %pad_maximum_fusion.6), channel_id=1, source_target_pairs={{0,1},{1,0},{2,3},{3,2},{4,5},{5,4},{6,7},{7,6},{8,9},{9,8},{10,11... | collective-permute-start | bytes 2359304 | tf_op jit(solution)/shard_map/ppermute | solution.py:199
  460.1 11.7 %collective-permute-start.29 = (bf16[128,1536]{1,0:T(8,128)(2,1)S(1)}, bf16[128,1536]{1,0:T(8,128)(2,1)S(1)}, u32[]{:S(2)}, u32[]{:S(2)}) collective-permute-start(bf16[128,1536]{1,0:T(8,128)(2,1)S(1)} %slice.210), channel_id=1, source_target_pairs={{0,2},{1,3},{2,0},{3,1},{4,6},{5,7},{6,4},{7,5},{8,10},{9,11},{10,... | collective-permute-start | bytes 1179656 | tf_op jit(solution)/shard_map/ppermute | solution.py:199
  470.3 20.3 %collective-permute-start.36 = (bf16[768,576]{0,1:T(8,128)(2,1)S(1)}, bf16[768,576]{0,1:T(8,128)(2,1)S(1)}, u32[]{:S(2)}, u32[]{:S(2)}) collective-permute-start(bf16[768,576]{0,1:T(8,128)(2,1)S(1)} %dynamic-slice_add_fusion), channel_id=1, source_target_pairs={{0,8},{4,12},{24,16},{28,20},{1,9},{5,13},{25,17},{29,21},{2,10},{... | collective-permute-start | bytes 2654216 | tf_op jit(solution)/shard_map/ppermute | solution.py:205
  473.2 19.2 %collective-permute-start.42 = (bf16[96,1536]{1,0:T(8,128)(2,1)S(1)}, bf16[96,1536]{1,0:T(8,128)(2,1)S(1)}, u32[]{:S(2)}, u32[]{:S(2)}) collective-permute-start(bf16[96,1536]{1,0:T(8,128)(2,1)S(1)} %constant_dynamic-slice_fusion), channel_id=1, source_target_pairs={{0,4},{4,0},{8,12},{12,8},{16,20},{20,16},{24,28},{28,24},{1,5},{5... | collective-permute-start | bytes 884744 | tf_op jit(solution)/shard_map/ppermute | solution.py:202
  474.8 14.6 %collective-permute-start.31 = (f32[3072]{0:T(1024)S(1)}, f32[3072]{0:T(1024)S(1)}, u32[]{:S(2)}, u32[]{:S(2)}) collective-permute-start(f32[3072]{0:T(1024)S(1)} %fusion.85), channel_id=1, source_target_pairs={{0,2},{1,3},{2,0},{3,1},{4,6},{5,7},{6,4},{7,5},{8,10},{9,11},{10,... | collective-permute-start | bytes 36872 | tf_op jit(solution)/shard_map/ppermute | solution.py:199
  490.0 22.8 %collective-permute-start.32 = (f32[3328]{0:T(1024)}, f32[3328]{0:T(1024)}, u32[]{:S(2)}, u32[]{:S(2)}) collective-permute-start(f32[3328]{0:T(1024)} %pad_maximum_fusion.8), channel_id=1, source_target_pairs={{0,4},{4,0},{8,12},{12,8},{16,20},{20,16},{24,28},{28,24},{1,5},{5... | collective-permute-start | bytes 39944 | tf_op jit(solution)/shard_map/ppermute | solution.py:202
  490.8 30.6 %collective-permute-start.37 = (bf16[768,576]{0,1:T(8,128)(2,1)S(1)}, bf16[768,576]{0,1:T(8,128)(2,1)}, u32[]{:S(2)}, u32[]{:S(2)}) collective-permute-start(bf16[768,576]{0,1:T(8,128)(2,1)S(1)} %add.201), channel_id=1, source_target_pairs={{8,16},{12,20},{16,8},{20,12},{9,17},{13,21},{17,9},{21,13},{10,18... | collective-permute-start | bytes 2654216 | tf_op jit(solution)/shard_map/ppermute | solution.py:205
  492.5 19.4 %collective-permute-start.43 = (bf16[96,1536]{1,0:T(8,128)(2,1)S(1)}, bf16[96,1536]{1,0:T(8,128)(2,1)S(1)}, u32[]{:S(2)}, u32[]{:S(2)}) collective-permute-start(bf16[96,1536]{1,0:T(8,128)(2,1)S(1)} %dynamic-slice_add_fusion.1), channel_id=1, source_target_pairs={{0,8},{4,12},{24,16},{28,20},{1,9},{5,13},{25,17},{29,21},{2,10},{... | collective-permute-start | bytes 884744 | tf_op jit(solution)/shard_map/ppermute | solution.py:205
  512.0 7.4 %collective-permute-start.44 = (bf16[96,1536]{1,0:T(8,128)(2,1)S(1)}, bf16[96,1536]{1,0:T(8,128)(2,1)S(1)}, u32[]{:S(2)}, u32[]{:S(2)}) collective-permute-start(bf16[96,1536]{1,0:T(8,128)(2,1)S(1)} %add.206), channel_id=1, source_target_pairs={{8,16},{12,20},{16,8},{20,12},{9,17},{13,21},{17,9},{21,13},{10,18... | collective-permute-start | bytes 884744 | tf_op jit(solution)/shard_map/ppermute | solution.py:205
  517.3 8.0 %collective-permute-start.34 = (f32[3328]{0:T(1024)S(1)}, f32[3328]{0:T(1024)S(1)}, u32[]{:S(2)}, u32[]{:S(2)}) collective-permute-start(f32[3328]{0:T(1024)S(1)} %add.196), channel_id=1, source_target_pairs={{0,16},{4,20},{8,24},{12,28},{16,0},{20,4},{24,8},{28,12},{1,17},{... | collective-permute-start | bytes 39944 | tf_op jit(solution)/shard_map/ppermute | solution.py:202
  520.2 12.1 %collective-permute-start.45 = (bf16[96,1536]{1,0:T(8,128)(2,1)}, bf16[96,1536]{1,0:T(8,128)(2,1)}, u32[]{:S(2)}, u32[]{:S(2)}) collective-permute-start(bf16[96,1536]{1,0:T(8,128)(2,1)} %add.207), channel_id=1, source_target_pairs={{8,0},{12,4},{16,24},{20,28},{9,1},{13,5},{17,25},{21,29},{10,2},{... | collective-permute-start | bytes 884744 | tf_op jit(solution)/shard_map/ppermute | solution.py:205
  522.9 25.3 %collective-permute-start.38 = (bf16[768,576]{0,1:T(8,128)(2,1)S(1)}, bf16[768,576]{0,1:T(8,128)(2,1)S(1)}, u32[]{:S(2)}, u32[]{:S(2)}) collective-permute-start(bf16[768,576]{0,1:T(8,128)(2,1)S(1)} %add.202), channel_id=1, source_target_pairs={{8,0},{12,4},{16,24},{20,28},{9,1},{13,5},{17,25},{21,29},{10,2},{... | collective-permute-start | bytes 2654216 | tf_op jit(solution)/shard_map/ppermute | solution.py:205
  533.3 16.8 %collective-permute-start.46 = (bf16[96,1536]{1,0:T(8,128)(2,1)S(1)}, bf16[96,1536]{1,0:T(8,128)(2,1)S(1)}, u32[]{:S(2)}, u32[]{:S(2)}) collective-permute-start(bf16[96,1536]{1,0:T(8,128)(2,1)S(1)} %broadcast_select_fusion.21), channel_id=1, source_target_pairs={{0,4},{4,0},{8,12},{12,8},{16,20},{20,16},{24,28},{28,24},{1,5},{5... | collective-permute-start | bytes 884744 | tf_op jit(solution)/shard_map/ppermute | solution.py:202
  548.2 18.7 %collective-permute-start.39 = (bf16[768,576]{0,1:T(8,128)(2,1)S(1)}, bf16[768,576]{0,1:T(8,128)(2,1)S(1)}, u32[]{:S(2)}, u32[]{:S(2)}) collective-permute-start(bf16[768,576]{0,1:T(8,128)(2,1)S(1)} %broadcast_select_fusion), channel_id=1, source_target_pairs={{0,4},{4,0},{8,12},{12,8},{16,20},{20,16},{24,28},{28,24},{1,5},{5... | collective-permute-start | bytes 2654216 | tf_op jit(solution)/shard_map/ppermute | solution.py:202
  (60 other events, 544.1 us)
